TPU v7x, 512 devices: a whole 4x4x16 slice. The times are simulated.
512 devices in a mesh: tm: 16 (over y, x), space: 32 (over z, core).
Axes of the slice: x: 4, y: 4, z: 16, core: 2. Of those that a mesh axis runs over, the one named last changes fastest.
Arguments:
- initial_state: float32 [3, 768, 256], P(None, 'space'), may hold values from -2 to 2
- c_guess: float32 [16, 3, 768, 256], P('tm', None, 'space'), may hold values from -2 to 2
- friction: float32 [768, 256], P('space'), may hold values from 0.05 to 1
Outputs:
- c_points: float32 [16, 3, 768, 256], P('tm', None, 'space')
- f_points: float32 [16, 3, 768, 256], P('tm', None, 'space')
All inputs are finite; a program needn't handle non-finite values.
Results may differ from a plain program's by a relative error of at most 0.00012.
Values sent between devices are 32-bit elements; how exact they have to be, the bound alone decides.
A program may use at most 64 MiB of HBM per device.

v0:
```python
import jax
import jax.numpy as jnp
from jax import lax
from jax.sharding import PartitionSpec as P

STEPS = 8


gravity = 2.0
coriolis = 0.5
viscosity = 0.5
time_step = 0.04


def with_halo(block, sides, width):
    for axis, dim in sides:
        count = lax.axis_size(axis)
        forward = [(i, i + 1) for i in range(count - 1)]
        forward.append((count - 1, 0))
        backward = [(target, source) for source, target in forward]
        low = lax.ppermute(
            lax.slice_in_dim(block, block.shape[dim] - width, None, axis=dim), axis, forward
        )
        high = lax.ppermute(lax.slice_in_dim(block, 0, width, axis=dim), axis, backward)
        block = jnp.concatenate([low, block, high], axis=dim)
    return block


def shifted(value, axis, by):
    size = lax.axis_size(axis)
    pairs = [(i, i + by) for i in range(size) if 0 <= i + by < size]
    return lax.ppermute(value, axis, pairs)


def joined_along(blocks, dim):
    blocks = jnp.moveaxis(blocks, 0, dim)
    dims = blocks.shape
    return blocks.reshape(*dims[:dim], dims[dim] * dims[dim + 1], *dims[dim + 2 :])


def sent_to_all(value, axis):
    copies = jnp.broadcast_to(value, (lax.axis_size(axis), *value.shape))
    return lax.all_to_all(copies, axis, split_axis=0, concat_axis=0, tiled=True)


def gathered_copies(value, axis, dim):
    return joined_along(sent_to_all(value, axis), dim)


def cut_neighbours(field):
    return (
        field[2:],
        field[:-2],
        jnp.roll(field, -1, 1)[1:-1],
        jnp.roll(field, 1, 1)[1:-1],
        field[1:-1],
    )


def spread(near):
    return near[0] + near[1] + near[2] + near[3] - 4.0 * near[4]


def tendency(fields, drag, neighbours):
    height = fields[0]
    row_vel = fields[1]
    col_vel = fields[2]
    height_near = neighbours(height)
    row_near = neighbours(row_vel)
    col_near = neighbours(col_vel)
    flux_row = neighbours((1.0 + height) * row_vel)
    flux_col = neighbours((1.0 + height) * col_vel)
    row_mid = row_near[4]
    col_mid = col_near[4]
    rate_height = -(
        0.5 * (flux_row[0] - flux_row[1]) + 0.5 * (flux_col[2] - flux_col[3])
    ) + viscosity * spread(height_near)
    rate_row = (
        -(
            row_mid * (0.5 * (row_near[0] - row_near[1]))
            + col_mid * (0.5 * (row_near[2] - row_near[3]))
        )
        - gravity * (0.5 * (height_near[0] - height_near[1]))
        + coriolis * col_mid
        - drag * row_mid
        + viscosity * spread(row_near)
    )
    rate_col = (
        -(
            row_mid * (0.5 * (col_near[0] - col_near[1]))
            + col_mid * (0.5 * (col_near[2] - col_near[3]))
        )
        - gravity * (0.5 * (height_near[2] - height_near[3]))
        - coriolis * row_mid
        - drag * col_mid
        + viscosity * spread(col_near)
    )
    return jnp.stack([rate_height, rate_row, rate_col])


def trim_rows(array, width):
    return array[..., width : array.shape[-2] - width, :]


def heun_step(fields, drag, size):
    slope_one = tendency(fields, drag[1:-1], cut_neighbours)
    midpoint = fields[:, 1:-1] + size * slope_one
    slope_two = tendency(midpoint, drag[2:-2], cut_neighbours)
    return fields[:, 2:-2] + 0.5 * size * (slope_one[:, 1:-1] + slope_two)


def advance(fields, drag_pad, step_count, layers, with_coarse):
    coarse = fields
    reaches = [layers] * (step_count // layers)
    if step_count % layers:
        reaches = reaches + [step_count % layers]
    for group, reach in enumerate(reaches):
        padded = with_halo(fields, (("space", 1),), 2 * reach)
        drag = trim_rows(drag_pad, 8 - 2 * reach)
        if with_coarse and group == 0:
            coarse = trim_rows(heun_step(padded, drag, STEPS * time_step), 2 * reach - 2)
        for repeat in range(reach):
            padded = heun_step(padded, drag, time_step)
            drag = trim_rows(drag, 2)
        fields = padded
    return (fields, coarse)


def body(initial_state, c_guess, friction):
    slice_index = lax.axis_index("tm")
    coarse_step = STEPS * time_step
    layers = 4
    drag_pad = with_halo(friction, (("space", 0),), 8)

    def earlier(fields):
        incoming = shifted(fields, "tm", 1)
        return jnp.where(slice_index == 0, initial_state, incoming)

    relaxed, unused = advance(earlier(c_guess[0]), drag_pad, STEPS, layers, False)
    fine_end, coarse_end = advance(earlier(relaxed), drag_pad, STEPS, layers, True)
    defect = fine_end - coarse_end
    defect_pad = with_halo(defect, (("space", 1),), 8)
    gathered = gathered_copies(defect_pad[None], "tm", 0)

    def group_fn(group, carry):
        current, owned = carry
        padded = with_halo(current, (("space", 1),), 8)
        drag = drag_pad
        for offset in range(4):
            turn = group * 4 + offset
            defect_now = trim_rows(
                lax.dynamic_index_in_dim(gathered, turn, 0, keepdims=False), 2 * offset + 2
            )
            padded = heun_step(padded, drag, coarse_step) + defect_now
            drag = trim_rows(drag, 2)
            owned = jnp.where(turn == slice_index, trim_rows(padded, 6 - 2 * offset), owned)
        return (padded, owned)

    unused_state, c_points = lax.fori_loop(
        0, lax.axis_size("tm") // 4, group_fn, (initial_state, jnp.zeros_like(defect))
    )
    f_points, unused_end = advance(earlier(c_points), drag_pad, STEPS - 1, layers, False)
    return (c_points[None], f_points[None])


def solution(mesh):
    placed = (P(None, "space", None), P("tm", None, "space", None), P("space", None))
    return jax.shard_map(
        body,
        mesh=mesh,
        in_specs=placed,
        out_specs=(P("tm", None, "space", None), P("tm", None, "space", None)),
        check_vma=False,
    )
```

profile of v0, /device:TPU:24, one launch (start us, length us, event | category | flops | bytes accessed | tf_op | source)
XLA Modules:
  0.0 197.2 jit_solution(16634545738339276303)
XLA Ops:
  0.6 0.7 fusion.2103
  1.4 8.9 %collective-permute-start.3 = (f32[8,256]{1,0:T(8,128)S(1)}, f32[8,256]{1,0:T(8,128)S(1)}, u32[]{:S(2)}, u32[]{:S(2)}) collective-permute-start(f32[8,256]{1,0:T(8,128)S(1)} %get-tuple-element.1470), channel_id=1, source_target_pairs={{1,0},{2,1},{3,2},{4,3},{5,4},{6,5},{7,6},{8,7},{9,8},{10,9},{11,1... | collective-permute-start | bytes 24584 | tf_op jit(solution)/shard_map/ppermute | solution.py:24
  10.3 3.4 %collective-permute-start.4 = (f32[3,24,256]{2,1,0:T(8,128)}, f32[3,24,256]{2,1,0:T(8,128)S(1)}, u32[]{:S(2)}, u32[]{:S(2)}) collective-permute-start(f32[3,24,256]{2,1,0:T(8,128)} %bitcast.5899), channel_id=1, source_target_pairs={{0,32},{32,64},{64,96},{96,128},{128,160},{160,192},{192,224},{224... | collective-permute-start | bytes 221192 | tf_op jit(solution)/shard_map/ppermute | solution.py:32
  13.7 0.7 constant_dynamic-update-slice_fusion.4
  14.5 4.4 %collective-permute-done.4 = f32[3,24,256]{2,1,0:T(8,128)S(1)} collective-permute-done((f32[3,24,256]{2,1,0:T(8,128)}, f32[3,24,256]{2,1,0:T(8,128)S(1)}, u32[]{:S(2)}, u32[]{:S(2)}) %collective-permute-start.4) | collective-permute-done | bytes 73760 | tf_op jit(solution)/shard_map/ppermute | solution.py:32
  18.9 2.9 %collective-permute-start.6 = (f32[3,8,256]{2,1,0:T(8,128)S(1)}, f32[3,8,256]{2,1,0:T(8,128)S(1)}, u32[]{:S(2)}, u32[]{:S(2)}) collective-permute-start(f32[3,8,256]{2,1,0:T(8,128)S(1)} %get-tuple-element.717), channel_id=1, source_target_pairs={{1,0},{2,1},{3,2},{4,3},{5,4},{6,5},{7,6},{8,7},{9,8},{10,9},{11,1... | collective-permute-start | bytes 73736 | tf_op jit(solution)/shard_map/ppermute | solution.py:24
  21.8 1.5 collective-permute-done.5
  29.0 0.1 fusion.1435
  30.0 0.1 fusion.1415
  31.4 3.0 %collective-permute-start.8 = (f32[3,8,256]{2,1,0:T(8,128)S(1)}, f32[3,8,256]{2,1,0:T(8,128)S(1)}, u32[]{:S(2)}, u32[]{:S(2)}) collective-permute-start(f32[3,8,256]{2,1,0:T(8,128)S(1)} %get-tuple-element.715), channel_id=1, source_target_pairs={{1,0},{2,1},{3,2},{4,3},{5,4},{6,5},{7,6},{8,7},{9,8},{10,9},{11,1... | collective-permute-start | bytes 73736 | tf_op jit(solution)/shard_map/ppermute | solution.py:24
  34.3 1.5 collective-permute-done.7
  36.6 0.1 fusion.709
  41.6 0.1 fusion.1355
  43.9 2.1 %collective-permute-start.9 = (f32[3,24,256]{2,1,0:T(8,128)S(1)}, f32[3,24,256]{2,1,0:T(8,128)S(1)}, u32[]{:S(2)}, u32[]{:S(2)}) collective-permute-start(f32[3,24,256]{2,1,0:T(8,128)S(1)} %fusion.289), channel_id=1, source_target_pairs={{0,32},{32,64},{64,96},{96,128},{128,160},{160,192},{192,224},{224... | collective-permute-start | bytes 221192 | tf_op jit(solution)/shard_map/ppermute | solution.py:32
  46.0 6.2 %collective-permute-done.9 = f32[3,24,256]{2,1,0:T(8,128)S(1)} collective-permute-done((f32[3,24,256]{2,1,0:T(8,128)S(1)}, f32[3,24,256]{2,1,0:T(8,128)S(1)}, u32[]{:S(2)}, u32[]{:S(2)}) %collective-permute-start.9) | collective-permute-done | bytes 73760 | tf_op jit(solution)/shard_map/ppermute | solution.py:32
  52.3 2.9 %collective-permute-start.11 = (f32[3,8,256]{2,1,0:T(8,128)S(1)}, f32[3,8,256]{2,1,0:T(8,128)S(1)}, u32[]{:S(2)}, u32[]{:S(2)}) collective-permute-start(f32[3,8,256]{2,1,0:T(8,128)S(1)} %get-tuple-element.713), channel_id=1, source_target_pairs={{1,0},{2,1},{3,2},{4,3},{5,4},{6,5},{7,6},{8,7},{9,8},{10,9},{11,1... | collective-permute-start | bytes 73736 | tf_op jit(solution)/shard_map/ppermute | solution.py:24
  55.3 1.5 collective-permute-done.10
  62.5 0.1 fusion.1275
  63.5 0.1 fusion.1255
  65.6 3.0 %collective-permute-start.13 = (f32[3,8,256]{2,1,0:T(8,128)S(1)}, f32[3,8,256]{2,1,0:T(8,128)S(1)}, u32[]{:S(2)}, u32[]{:S(2)}) collective-permute-start(f32[3,8,256]{2,1,0:T(8,128)S(1)} %get-tuple-element.711), channel_id=1, source_target_pairs={{1,0},{2,1},{3,2},{4,3},{5,4},{6,5},{7,6},{8,7},{9,8},{10,9},{11,1... | collective-permute-start | bytes 73736 | tf_op jit(solution)/shard_map/ppermute | solution.py:24
  68.9 1.2 collective-permute-done.12
  74.8 0.1 fusion.1215
  76.8 0.1 fusion.1175
  78.2 3.0 %collective-permute-start.15 = (f32[3,8,256]{2,1,0:T(8,128)S(1)}, f32[3,8,256]{2,1,0:T(8,128)S(1)}, u32[]{:S(2)}, u32[]{:S(2)}) collective-permute-start(f32[3,8,256]{2,1,0:T(8,128)S(1)} %get-tuple-element.709), channel_id=1, source_target_pairs={{1,0},{2,1},{3,2},{4,3},{5,4},{6,5},{7,6},{8,7},{9,8},{10,9},{11,1... | collective-permute-start | bytes 73736 | tf_op jit(solution)/shard_map/ppermute | solution.py:24
  81.2 1.5 collective-permute-done.14
  82.7 1.4 broadcast_in_dim.14
  84.1 4.8 %all-to-all-start = ((f32[16,1,3,40,256]{4,3,2,1,0:T(8,128)}), f32[16,1,3,40,256]{4,3,2,1,0:T(8,128)S(1)}, u32[]{:S(2)}, u32[]{:S(2)}) async-start(f32[16,1,3,40,256]{4,3,2,1,0:T(8,128)} %broadcast_in_dim.14), calls=%async_computation | async-start | bytes 3932160 | tf_op jit(solution)/shard_map/all_to_all | solution.py:43
  88.9 23.1 %all-to-all-done = f32[16,1,3,40,256]{4,3,2,1,0:T(8,128)S(1)} async-done(((f32[16,1,3,40,256]{4,3,2,1,0:T(8,128)}), f32[16,1,3,40,256]{4,3,2,1,0:T(8,128)S(1)}, u32[]{:S(2)}, u32[]{:S(2)}) %all-to-all-start) | async-done | bytes 1966112 | tf_op jit(solution)/shard_map/all_to_all | solution.py:43
  112.1 53.0 %while.19 = (s32[]{:T(128)}, f32[3,24,256]{2,1,0:T(8,128)S(1)}, f32[3,24,256]{2,1,0:T(8,128)S(1)}, f32[40,256]{1,0:T(8,128)S(1)}, f32[16,3,40,256]{3,2,1,0:T(8,1...) while((s32[]{:T(128)}, f32[3,24,256]{2,1,0:T(8,128)S(1)}, ...), condition=%wide.region_1.2_spmd.clone, body=%wide.region_0.1_spmd.clone.sunk | while | flops 5304343 | bytes 20316628 | solution.py:159
  112.1 5.9 %collective-permute-start.1 = (f32[3,8,256]{2,1,0:T(8,128)S(1)}, f32[3,8,256]{2,1,0:T(8,128)S(1)}, u32[]{:S(2)}, u32[]{:S(2)}) collective-permute-start(f32[3,8,256]{2,1,0:T(8,128)S(1)} %get-tuple-element.1699), channel_id=1, source_target_pairs={{1,0},{2,1},{3,2},{4,3},{5,4},{6,5},{7,6},{8,7},{9,8},{10,9},{11,1... | collective-permute-start | bytes 73736 | tf_op jit(solution)/shard_map/while/body/eval_jaxpr/ppermute | solution.py:24
  118.1 1.4 collective-permute-done
  127.6 2.9 %collective-permute-start.1 = (f32[3,8,256]{2,1,0:T(8,128)S(1)}, f32[3,8,256]{2,1,0:T(8,128)S(1)}, u32[]{:S(2)}, u32[]{:S(2)}) collective-permute-start(f32[3,8,256]{2,1,0:T(8,128)S(1)} %get-tuple-element.1699), channel_id=1, source_target_pairs={{1,0},{2,1},{3,2},{4,3},{5,4},{6,5},{7,6},{8,7},{9,8},{10,9},{11,1... | collective-permute-start | bytes 73736 | tf_op jit(solution)/shard_map/while/body/eval_jaxpr/ppermute | solution.py:24
  130.6 1.4 collective-permute-done
  140.1 2.9 %collective-permute-start.1 = (f32[3,8,256]{2,1,0:T(8,128)S(1)}, f32[3,8,256]{2,1,0:T(8,128)S(1)}, u32[]{:S(2)}, u32[]{:S(2)}) collective-permute-start(f32[3,8,256]{2,1,0:T(8,128)S(1)} %get-tuple-element.1699), channel_id=1, source_target_pairs={{1,0},{2,1},{3,2},{4,3},{5,4},{6,5},{7,6},{8,7},{9,8},{10,9},{11,1... | collective-permute-start | bytes 73736 | tf_op jit(solution)/shard_map/while/body/eval_jaxpr/ppermute | solution.py:24
  143.1 1.4 collective-permute-done
  152.6 2.9 %collective-permute-start.1 = (f32[3,8,256]{2,1,0:T(8,128)S(1)}, f32[3,8,256]{2,1,0:T(8,128)S(1)}, u32[]{:S(2)}, u32[]{:S(2)}) collective-permute-start(f32[3,8,256]{2,1,0:T(8,128)S(1)} %get-tuple-element.1699), channel_id=1, source_target_pairs={{1,0},{2,1},{3,2},{4,3},{5,4},{6,5},{7,6},{8,7},{9,8},{10,9},{11,1... | collective-permute-start | bytes 73736 | tf_op jit(solution)/shard_map/while/body/eval_jaxpr/ppermute | solution.py:24
  155.6 1.4 collective-permute-done
  165.1 2.1 %collective-permute-start.16 = (f32[3,24,256]{2,1,0:T(8,128)S(1)}, f32[3,24,256]{2,1,0:T(8,128)S(1)}, u32[]{:S(2)}, u32[]{:S(2)}) collective-permute-start(f32[3,24,256]{2,1,0:T(8,128)S(1)} %get-tuple-element.197), channel_id=1, source_target_pairs={{0,32},{32,64},{64,96},{96,128},{128,160},{160,192},{192,224},{224... | collective-permute-start | bytes 221192 | tf_op jit(solution)/shard_map/ppermute | solution.py:32
  167.2 6.2 %collective-permute-done.16 = f32[3,24,256]{2,1,0:T(8,128)S(1)} collective-permute-done((f32[3,24,256]{2,1,0:T(8,128)S(1)}, f32[3,24,256]{2,1,0:T(8,128)S(1)}, u32[]{:S(2)}, u32[]{:S(2)}) %collective-permute-start.16) | collective-permute-done | bytes 73760 | tf_op jit(solution)/shard_map/ppermute | solution.py:32
  173.5 2.9 %collective-permute-start.18 = (f32[3,8,256]{2,1,0:T(8,128)S(1)}, f32[3,8,256]{2,1,0:T(8,128)S(1)}, u32[]{:S(2)}, u32[]{:S(2)}) collective-permute-start(f32[3,8,256]{2,1,0:T(8,128)S(1)} %get-tuple-element.707), channel_id=1, source_target_pairs={{1,0},{2,1},{3,2},{4,3},{5,4},{6,5},{7,6},{8,7},{9,8},{10,9},{11,1... | collective-permute-start | bytes 73736 | tf_op jit(solution)/shard_map/ppermute | solution.py:24
  176.4 1.5 collective-permute-done.17
  178.7 0.1 fusion.509
  183.7 0.1 fusion.1115
  184.7 0.1 fusion.1095
  186.1 3.0 %collective-permute-start.20 = (f32[3,6,256]{2,1,0:T(8,128)S(1)}, f32[3,6,256]{2,1,0:T(8,128)S(1)}, u32[]{:S(2)}, u32[]{:S(2)}) collective-permute-start(f32[3,6,256]{2,1,0:T(8,128)S(1)} %get-tuple-element.705), channel_id=1, source_target_pairs={{1,0},{2,1},{3,2},{4,3},{5,4},{6,5},{7,6},{8,7},{9,8},{10,9},{11,1... | collective-permute-start | bytes 55304 | tf_op jit(solution)/shard_map/ppermute | solution.py:24
  189.0 1.5 collective-permute-done.19
  194.2 0.1 fusion.1035
  196.5 0.7 fusion.279
  (1155 shorter events, 75.8 us)
Async XLA Ops:
  1.3 12.3 %collective-permute-start.2 = (f32[8,256]{1,0:T(8,128)S(1)}, f32[8,256]{1,0:T(8,128)S(1)}, u32[]{:S(2)}, u32[]{:S(2)}) collective-permute-start(f32[8,256]{1,0:T(8,128)S(1)} %get-tuple-element.1471), channel_id=1, source_target_pairs={{0,1},{1,2},{2,3},{3,4},{4,5},{5,6},{6,7},{7,8},{8,9},{9,10},{10,1... | collective-permute-start | bytes 24584 | tf_op jit(solution)/shard_map/ppermute | solution.py:21
  1.4 20.5 %collective-permute-start.3 = (f32[8,256]{1,0:T(8,128)S(1)}, f32[8,256]{1,0:T(8,128)S(1)}, u32[]{:S(2)}, u32[]{:S(2)}) collective-permute-start(f32[8,256]{1,0:T(8,128)S(1)} %get-tuple-element.1470), channel_id=1, source_target_pairs={{1,0},{2,1},{3,2},{4,3},{5,4},{6,5},{7,6},{8,7},{9,8},{10,9},{11,1... | collective-permute-start | bytes 24584 | tf_op jit(solution)/shard_map/ppermute | solution.py:24
  10.3 8.6 %collective-permute-start.4 = (f32[3,24,256]{2,1,0:T(8,128)}, f32[3,24,256]{2,1,0:T(8,128)S(1)}, u32[]{:S(2)}, u32[]{:S(2)}) collective-permute-start(f32[3,24,256]{2,1,0:T(8,128)} %bitcast.5899), channel_id=1, source_target_pairs={{0,32},{32,64},{64,96},{96,128},{128,160},{160,192},{192,224},{224... | collective-permute-start | bytes 221192 | tf_op jit(solution)/shard_map/ppermute | solution.py:32
  18.9 4.5 %collective-permute-start.5 = (f32[3,8,256]{2,1,0:T(8,128)S(1)}, f32[3,8,256]{2,1,0:T(8,128)S(1)}, u32[]{:S(2)}, u32[]{:S(2)}) collective-permute-start(f32[3,8,256]{2,1,0:T(8,128)S(1)} %get-tuple-element.716), channel_id=1, source_target_pairs={{0,1},{1,2},{2,3},{3,4},{4,5},{5,6},{6,7},{7,8},{8,9},{9,10},{10,1... | collective-permute-start | bytes 73736 | tf_op jit(solution)/shard_map/ppermute | solution.py:21
  18.9 4.5 %collective-permute-start.6 = (f32[3,8,256]{2,1,0:T(8,128)S(1)}, f32[3,8,256]{2,1,0:T(8,128)S(1)}, u32[]{:S(2)}, u32[]{:S(2)}) collective-permute-start(f32[3,8,256]{2,1,0:T(8,128)S(1)} %get-tuple-element.717), channel_id=1, source_target_pairs={{1,0},{2,1},{3,2},{4,3},{5,4},{6,5},{7,6},{8,7},{9,8},{10,9},{11,1... | collective-permute-start | bytes 73736 | tf_op jit(solution)/shard_map/ppermute | solution.py:24
  29.3 1.6 copy-start.2
  31.3 4.5 %collective-permute-start.7 = (f32[3,8,256]{2,1,0:T(8,128)S(1)}, f32[3,8,256]{2,1,0:T(8,128)S(1)}, u32[]{:S(2)}, u32[]{:S(2)}) collective-permute-start(f32[3,8,256]{2,1,0:T(8,128)S(1)} %get-tuple-element.714), channel_id=1, source_target_pairs={{0,1},{1,2},{2,3},{3,4},{4,5},{5,6},{6,7},{7,8},{8,9},{9,10},{10,1... | collective-permute-start | bytes 73736 | tf_op jit(solution)/shard_map/ppermute | solution.py:21
  31.4 4.5 %collective-permute-start.8 = (f32[3,8,256]{2,1,0:T(8,128)S(1)}, f32[3,8,256]{2,1,0:T(8,128)S(1)}, u32[]{:S(2)}, u32[]{:S(2)}) collective-permute-start(f32[3,8,256]{2,1,0:T(8,128)S(1)} %get-tuple-element.715), channel_id=1, source_target_pairs={{1,0},{2,1},{3,2},{4,3},{5,4},{6,5},{7,6},{8,7},{9,8},{10,9},{11,1... | collective-permute-start | bytes 73736 | tf_op jit(solution)/shard_map/ppermute | solution.py:24
  42.6 9.7 %copy-start = (f32[3,24,256]{2,1,0:T(8,128)S(1)}, f32[3,24,256]{2,1,0:T(8,128)}, u32[]{:S(2)}) copy-start(f32[3,24,256]{2,1,0:T(8,128)} %param.5) | copy-start | bytes 221188
  43.9 8.4 %collective-permute-start.9 = (f32[3,24,256]{2,1,0:T(8,128)S(1)}, f32[3,24,256]{2,1,0:T(8,128)S(1)}, u32[]{:S(2)}, u32[]{:S(2)}) collective-permute-start(f32[3,24,256]{2,1,0:T(8,128)S(1)} %fusion.289), channel_id=1, source_target_pairs={{0,32},{32,64},{64,96},{96,128},{128,160},{160,192},{192,224},{224... | collective-permute-start | bytes 221192 | tf_op jit(solution)/shard_map/ppermute | solution.py:32
  52.3 4.5 %collective-permute-start.10 = (f32[3,8,256]{2,1,0:T(8,128)S(1)}, f32[3,8,256]{2,1,0:T(8,128)S(1)}, u32[]{:S(2)}, u32[]{:S(2)}) collective-permute-start(f32[3,8,256]{2,1,0:T(8,128)S(1)} %get-tuple-element.712), channel_id=1, source_target_pairs={{0,1},{1,2},{2,3},{3,4},{4,5},{5,6},{6,7},{7,8},{8,9},{9,10},{10,1... | collective-permute-start | bytes 73736 | tf_op jit(solution)/shard_map/ppermute | solution.py:21
  52.3 4.5 %collective-permute-start.11 = (f32[3,8,256]{2,1,0:T(8,128)S(1)}, f32[3,8,256]{2,1,0:T(8,128)S(1)}, u32[]{:S(2)}, u32[]{:S(2)}) collective-permute-start(f32[3,8,256]{2,1,0:T(8,128)S(1)} %get-tuple-element.713), channel_id=1, source_target_pairs={{1,0},{2,1},{3,2},{4,3},{5,4},{6,5},{7,6},{8,7},{9,8},{10,9},{11,1... | collective-permute-start | bytes 73736 | tf_op jit(solution)/shard_map/ppermute | solution.py:24
  65.6 4.5 %collective-permute-start.12 = (f32[3,8,256]{2,1,0:T(8,128)S(1)}, f32[3,8,256]{2,1,0:T(8,128)S(1)}, u32[]{:S(2)}, u32[]{:S(2)}) collective-permute-start(f32[3,8,256]{2,1,0:T(8,128)S(1)} %get-tuple-element.710), channel_id=1, source_target_pairs={{0,1},{1,2},{2,3},{3,4},{4,5},{5,6},{6,7},{7,8},{8,9},{9,10},{10,1... | collective-permute-start | bytes 73736 | tf_op jit(solution)/shard_map/ppermute | solution.py:21
  65.6 4.5 %collective-permute-start.13 = (f32[3,8,256]{2,1,0:T(8,128)S(1)}, f32[3,8,256]{2,1,0:T(8,128)S(1)}, u32[]{:S(2)}, u32[]{:S(2)}) collective-permute-start(f32[3,8,256]{2,1,0:T(8,128)S(1)} %get-tuple-element.711), channel_id=1, source_target_pairs={{1,0},{2,1},{3,2},{4,3},{5,4},{6,5},{7,6},{8,7},{9,8},{10,9},{11,1... | collective-permute-start | bytes 73736 | tf_op jit(solution)/shard_map/ppermute | solution.py:24
  78.2 4.5 %collective-permute-start.14 = (f32[3,8,256]{2,1,0:T(8,128)S(1)}, f32[3,8,256]{2,1,0:T(8,128)S(1)}, u32[]{:S(2)}, u32[]{:S(2)}) collective-permute-start(f32[3,8,256]{2,1,0:T(8,128)S(1)} %get-tuple-element.708), channel_id=1, source_target_pairs={{0,1},{1,2},{2,3},{3,4},{4,5},{5,6},{6,7},{7,8},{8,9},{9,10},{10,1... | collective-permute-start | bytes 73736 | tf_op jit(solution)/shard_map/ppermute | solution.py:21
  78.2 4.5 %collective-permute-start.15 = (f32[3,8,256]{2,1,0:T(8,128)S(1)}, f32[3,8,256]{2,1,0:T(8,128)S(1)}, u32[]{:S(2)}, u32[]{:S(2)}) collective-permute-start(f32[3,8,256]{2,1,0:T(8,128)S(1)} %get-tuple-element.709), channel_id=1, source_target_pairs={{1,0},{2,1},{3,2},{4,3},{5,4},{6,5},{7,6},{8,7},{9,8},{10,9},{11,1... | collective-permute-start | bytes 73736 | tf_op jit(solution)/shard_map/ppermute | solution.py:24
  84.1 28.0 %copy-start.1 = (f32[3,24,256]{2,1,0:T(8,128)S(1)}, f32[3,24,256]{2,1,0:T(8,128)}, u32[]{:S(2)}) copy-start(f32[3,24,256]{2,1,0:T(8,128)} %param.5) | copy-start | bytes 221188
  84.1 27.9 %all-to-all-start = ((f32[16,1,3,40,256]{4,3,2,1,0:T(8,128)}), f32[16,1,3,40,256]{4,3,2,1,0:T(8,128)S(1)}, u32[]{:S(2)}, u32[]{:S(2)}) async-start(f32[16,1,3,40,256]{4,3,2,1,0:T(8,128)} %broadcast_in_dim.14), calls=%async_computation | async-start | bytes 3932160 | tf_op jit(solution)/shard_map/all_to_all | solution.py:43
  112.1 7.4 %collective-permute-start = (f32[3,8,256]{2,1,0:T(8,128)S(1)}, f32[3,8,256]{2,1,0:T(8,128)S(1)}, u32[]{:S(2)}, u32[]{:S(2)}) collective-permute-start(f32[3,8,256]{2,1,0:T(8,128)S(1)} %get-tuple-element.1698), channel_id=1, source_target_pairs={{0,1},{1,2},{2,3},{3,4},{4,5},{5,6},{6,7},{7,8},{8,9},{9,10},{10,1... | collective-permute-start | bytes 73736 | tf_op jit(solution)/shard_map/while/body/eval_jaxpr/ppermute | solution.py:21
  112.1 7.4 %collective-permute-start.1 = (f32[3,8,256]{2,1,0:T(8,128)S(1)}, f32[3,8,256]{2,1,0:T(8,128)S(1)}, u32[]{:S(2)}, u32[]{:S(2)}) collective-permute-start(f32[3,8,256]{2,1,0:T(8,128)S(1)} %get-tuple-element.1699), channel_id=1, source_target_pairs={{1,0},{2,1},{3,2},{4,3},{5,4},{6,5},{7,6},{8,7},{9,8},{10,9},{11,1... | collective-permute-start | bytes 73736 | tf_op jit(solution)/shard_map/while/body/eval_jaxpr/ppermute | solution.py:24
  127.5 4.5 %collective-permute-start = (f32[3,8,256]{2,1,0:T(8,128)S(1)}, f32[3,8,256]{2,1,0:T(8,128)S(1)}, u32[]{:S(2)}, u32[]{:S(2)}) collective-permute-start(f32[3,8,256]{2,1,0:T(8,128)S(1)} %get-tuple-element.1698), channel_id=1, source_target_pairs={{0,1},{1,2},{2,3},{3,4},{4,5},{5,6},{6,7},{7,8},{8,9},{9,10},{10,1... | collective-permute-start | bytes 73736 | tf_op jit(solution)/shard_map/while/body/eval_jaxpr/ppermute | solution.py:21
  127.6 4.4 %collective-permute-start.1 = (f32[3,8,256]{2,1,0:T(8,128)S(1)}, f32[3,8,256]{2,1,0:T(8,128)S(1)}, u32[]{:S(2)}, u32[]{:S(2)}) collective-permute-start(f32[3,8,256]{2,1,0:T(8,128)S(1)} %get-tuple-element.1699), channel_id=1, source_target_pairs={{1,0},{2,1},{3,2},{4,3},{5,4},{6,5},{7,6},{8,7},{9,8},{10,9},{11,1... | collective-permute-start | bytes 73736 | tf_op jit(solution)/shard_map/while/body/eval_jaxpr/ppermute | solution.py:24
  140.0 4.5 %collective-permute-start = (f32[3,8,256]{2,1,0:T(8,128)S(1)}, f32[3,8,256]{2,1,0:T(8,128)S(1)}, u32[]{:S(2)}, u32[]{:S(2)}) collective-permute-start(f32[3,8,256]{2,1,0:T(8,128)S(1)} %get-tuple-element.1698), channel_id=1, source_target_pairs={{0,1},{1,2},{2,3},{3,4},{4,5},{5,6},{6,7},{7,8},{8,9},{9,10},{10,1... | collective-permute-start | bytes 73736 | tf_op jit(solution)/shard_map/while/body/eval_jaxpr/ppermute | solution.py:21
  140.1 4.5 %collective-permute-start.1 = (f32[3,8,256]{2,1,0:T(8,128)S(1)}, f32[3,8,256]{2,1,0:T(8,128)S(1)}, u32[]{:S(2)}, u32[]{:S(2)}) collective-permute-start(f32[3,8,256]{2,1,0:T(8,128)S(1)} %get-tuple-element.1699), channel_id=1, source_target_pairs={{1,0},{2,1},{3,2},{4,3},{5,4},{6,5},{7,6},{8,7},{9,8},{10,9},{11,1... | collective-permute-start | bytes 73736 | tf_op jit(solution)/shard_map/while/body/eval_jaxpr/ppermute | solution.py:24
  152.6 4.5 %collective-permute-start = (f32[3,8,256]{2,1,0:T(8,128)S(1)}, f32[3,8,256]{2,1,0:T(8,128)S(1)}, u32[]{:S(2)}, u32[]{:S(2)}) collective-permute-start(f32[3,8,256]{2,1,0:T(8,128)S(1)} %get-tuple-element.1698), channel_id=1, source_target_pairs={{0,1},{1,2},{2,3},{3,4},{4,5},{5,6},{6,7},{7,8},{8,9},{9,10},{10,1... | collective-permute-start | bytes 73736 | tf_op jit(solution)/shard_map/while/body/eval_jaxpr/ppermute | solution.py:21
  152.6 4.5 %collective-permute-start.1 = (f32[3,8,256]{2,1,0:T(8,128)S(1)}, f32[3,8,256]{2,1,0:T(8,128)S(1)}, u32[]{:S(2)}, u32[]{:S(2)}) collective-permute-start(f32[3,8,256]{2,1,0:T(8,128)S(1)} %get-tuple-element.1699), channel_id=1, source_target_pairs={{1,0},{2,1},{3,2},{4,3},{5,4},{6,5},{7,6},{8,7},{9,8},{10,9},{11,1... | collective-permute-start | bytes 73736 | tf_op jit(solution)/shard_map/while/body/eval_jaxpr/ppermute | solution.py:24
  165.1 13.9 %copy-start.3 = (f32[3,24,256]{2,1,0:T(8,128)}, f32[3,24,256]{2,1,0:T(8,128)S(1)}, u32[]{:S(2)}) copy-start(f32[3,24,256]{2,1,0:T(8,128)S(1)} %get-tuple-element.197) | copy-start | bytes 221188
  165.1 8.4 %collective-permute-start.16 = (f32[3,24,256]{2,1,0:T(8,128)S(1)}, f32[3,24,256]{2,1,0:T(8,128)S(1)}, u32[]{:S(2)}, u32[]{:S(2)}) collective-permute-start(f32[3,24,256]{2,1,0:T(8,128)S(1)} %get-tuple-element.197), channel_id=1, source_target_pairs={{0,32},{32,64},{64,96},{96,128},{128,160},{160,192},{192,224},{224... | collective-permute-start | bytes 221192 | tf_op jit(solution)/shard_map/ppermute | solution.py:32
  173.5 4.5 %collective-permute-start.17 = (f32[3,8,256]{2,1,0:T(8,128)S(1)}, f32[3,8,256]{2,1,0:T(8,128)S(1)}, u32[]{:S(2)}, u32[]{:S(2)}) collective-permute-start(f32[3,8,256]{2,1,0:T(8,128)S(1)} %get-tuple-element.706), channel_id=1, source_target_pairs={{0,1},{1,2},{2,3},{3,4},{4,5},{5,6},{6,7},{7,8},{8,9},{9,10},{10,1... | collective-permute-start | bytes 73736 | tf_op jit(solution)/shard_map/ppermute | solution.py:21
  173.5 4.5 %collective-permute-start.18 = (f32[3,8,256]{2,1,0:T(8,128)S(1)}, f32[3,8,256]{2,1,0:T(8,128)S(1)}, u32[]{:S(2)}, u32[]{:S(2)}) collective-permute-start(f32[3,8,256]{2,1,0:T(8,128)S(1)} %get-tuple-element.707), channel_id=1, source_target_pairs={{1,0},{2,1},{3,2},{4,3},{5,4},{6,5},{7,6},{8,7},{9,8},{10,9},{11,1... | collective-permute-start | bytes 73736 | tf_op jit(solution)/shard_map/ppermute | solution.py:24
  186.0 4.5 %collective-permute-start.19 = (f32[3,6,256]{2,1,0:T(8,128)S(1)}, f32[3,6,256]{2,1,0:T(8,128)S(1)}, u32[]{:S(2)}, u32[]{:S(2)}) collective-permute-start(f32[3,6,256]{2,1,0:T(8,128)S(1)} %get-tuple-element.704), channel_id=1, source_target_pairs={{0,1},{1,2},{2,3},{3,4},{4,5},{5,6},{6,7},{7,8},{8,9},{9,10},{10,1... | collective-permute-start | bytes 55304 | tf_op jit(solution)/shard_map/ppermute | solution.py:21
  186.1 4.5 %collective-permute-start.20 = (f32[3,6,256]{2,1,0:T(8,128)S(1)}, f32[3,6,256]{2,1,0:T(8,128)S(1)}, u32[]{:S(2)}, u32[]{:S(2)}) collective-permute-start(f32[3,6,256]{2,1,0:T(8,128)S(1)} %get-tuple-element.705), channel_id=1, source_target_pairs={{1,0},{2,1},{3,2},{4,3},{5,4},{6,5},{7,6},{8,7},{9,8},{10,9},{11,1... | collective-permute-start | bytes 55304 | tf_op jit(solution)/shard_map/ppermute | solution.py:24
where the time goes:
time: 198 us; the launch traced here: 197 us
  starting transfers between devices  57 us (29%)
  waiting for transfers between devices  56 us (28%)
  local copies, waits for them, and re-layouts  50.4 us (25%)
  other arithmetic  29.9 us (15%)
  between operations  2.55 us (1%)
    ppermute x12, starting transfers between devices, with_halo(): lax.ppermute(lax.slice_in_dim(block, 0, width, axis=dim), axis, backward)  44.2 us
    slice x464, local copies, waits for them, and re-layouts, cut_neighbours(): jnp.roll(field, 1, 1)[1:-1]  34.7 us
    another operation x241, other arithmetic, tendency(): return jnp.stack([rate_height, rate_row, rate_col])  25.7 us
    all_to_all x1, waiting for transfers between devices, sent_to_all(): return lax.all_to_all(copies, axis, split_axis=0, concat_axis=0, tiled=True)  23.1 us
    ppermute x3, waiting for transfers between devices, shifted(): return lax.ppermute(value, axis, pairs)  16.8 us
    ppermute x12, waiting for transfers between devices, with_halo(): lax.ppermute(lax.slice_in_dim(block, block.shape[dim] - width, None, axis...  15.9 us
    slice x158, local copies, waits for them, and re-layouts, cut_neighbours(): jnp.roll(field, -1, 1)[1:-1]  11.7 us
    ppermute x3, starting transfers between devices, shifted(): return lax.ppermute(value, axis, pairs)  7.63 us
  transfers between devices with their start and end apart: 28, of which 15 were waited for; matrix products, arithmetic and copies ran while one was open for 1% of the time, Pallas kernels for 0%

commit v1 on v0

v1 whole, which is shorter than its diff:
```python
import functools

import jax
import jax.numpy as jnp
from jax import lax
from jax.experimental import pallas as pl
from jax.experimental.pallas import tpu as pltpu
from jax.sharding import PartitionSpec as P

STEPS = 8
time_step = 0.04
coarse_step = STEPS * time_step
MESH = pl.DeviceIdType.MESH

HALO = 16
LANES = 128
BASE = 8
LOOK = 3


def shifted_lanes(pair, by, edge):
    turned = [pltpu.roll(part, by % LANES, 1) for part in pair]
    return [jnp.where(edge, turned[1], turned[0]), jnp.where(edge, turned[0], turned[1])]


def advanced(src, drag, row, scale, weight, low_edge, high_edge):
    alpha = weight * scale
    here, below, above, right, left = [], [], [], [], []
    for field in range(3):
        here.append([src[field, half, pl.ds(row, 8), :] for half in (0, 1)])
        below.append([src[field, half, pl.ds(row + 1, 8), :] for half in (0, 1)])
        above.append([src[field, half, pl.ds(row - 1, 8), :] for half in (0, 1)])
        right.append(shifted_lanes(here[field], -1, high_edge))
        left.append(shifted_lanes(here[field], 1, low_edge))
    out = [[], [], []]
    for half in (0, 1):
        e, u, w = (here[field][half] for field in range(3))
        e_ip, u_ip, w_ip = (below[field][half] for field in range(3))
        e_im, u_im, w_im = (above[field][half] for field in range(3))
        e_jp, u_jp, w_jp = (right[field][half] for field in range(3))
        e_jm, u_jm, w_jm = (left[field][half] for field in range(3))
        along = (e_ip - (1.0 + e_ip) * u_ip) + (e_im + (1.0 + e_im) * u_im)
        across = (e_jp - (1.0 + e_jp) * w_jp) + (e_jm + (1.0 + e_jm) * w_jm)
        out[0].append((weight - 4.0 * alpha) * e + alpha * (along + across))
        au = alpha * u
        aw = alpha * w
        u_low, u_high, w_low, w_high = alpha - au, alpha + au, alpha - aw, alpha + aw
        keep = drag[half, pl.ds(row, 8), :]
        out[1].append(
            (u_ip * u_low + u_im * u_high)
            + (u_jp * w_low + u_jm * w_high)
            + ((aw - (2.0 * alpha) * (e_ip - e_im)) + keep * u)
        )
        out[2].append(
            (w_ip * u_low + w_im * u_high)
            + (w_jp * w_low + w_jm * w_high)
            + (keep * w - (au + (2.0 * alpha) * (e_jp - e_jm)))
        )
    return out, here


def kernel(
    times, strips, rows,
    init_ref, guess_ref, fric_ref, c_ref, f_ref,
    first, second, third, fourth, mid, drag_raw, drags, gained, defects, own_defect, coarse_end,
    halo_send, halo_recv, fric_send, fric_recv, init_send, start_recv, own_recv,
    second_send, second_recv, defect_send, defect_recv, edge_send, edge_recv,
    hand_send, fourth_send, fourth_recv,
):
    half = times // 2
    t = lax.axis_index("tm")
    z = lax.axis_index("space")
    up = lax.rem(z + strips - 1, strips)
    down = lax.rem(z + 1, strips)
    group = t // half
    place = lax.rem(t, half)
    slot = lax.rem(t + 2, times)
    slot_group = slot // half
    slot_place = lax.rem(slot, half)

    own = pl.ds(BASE + HALO, rows)
    upper = pl.ds(BASE, HALO)
    lower = pl.ds(BASE + HALO + rows, HALO)
    own_first = pl.ds(BASE + HALO, HALO)
    own_last = pl.ds(BASE + rows, HALO)

    def remote(src, dst, send, recv, target):
        return pltpu.make_async_remote_copy(
            src_ref=src, dst_ref=dst, send_sem=send, recv_sem=recv, device_id=target, device_id_type=MESH
        )

    def edges_of(ref, send, recv):
        return (
            remote(ref.at[:, :, own_last, :], ref.at[:, :, upper, :], send.at[0], recv.at[0], (t, down)),
            remote(ref.at[:, :, own_first, :], ref.at[:, :, lower, :], send.at[1], recv.at[1], (t, up)),
        )

    barrier = pltpu.get_barrier_semaphore()

    def greet(*target):
        pl.semaphore_signal(barrier, inc=1, device_id=target, device_id_type=MESH)

    greet(t, up)
    greet(t, down)
    for other in range(1, times):
        greet(lax.rem(t + other, times), z)

    @pl.when(t == half - 1)
    def _():
        for later in range(half, times):
            greet(later, up)
            greet(later, down)

    @pl.when(t >= half)
    def _():
        greet(half - 1, up)
        greet(half - 1, down)

    is_last = t == times - 1
    for field in range(3):
        for side in (0, 1):
            cols = slice(side * LANES, (side + 1) * LANES)
            first[field, side, own, :] = jnp.where(is_last, init_ref[field, :, cols], guess_ref[0, field, :, cols])
    for side in (0, 1):
        drag_raw[0, side, own, :] = fric_ref[:, side * LANES : (side + 1) * LANES]

    @pl.when(t < half)
    def _():
        for field in range(3):
            for side in (0, 1):
                third[field, side, own, :] = init_ref[field, :, side * LANES : (side + 1) * LANES]

    greeted = jnp.where(t == half - 1, 2 * half, jnp.where(t >= half, 2, 0))
    pl.semaphore_wait(barrier, times + 1 + greeted)

    first_edges = edges_of(first, halo_send, halo_recv)
    drag_edges = edges_of(drag_raw, fric_send, fric_recv)
    third_edges = edges_of(third, init_send, start_recv)
    for copy in first_edges + drag_edges:
        copy.start()

    @pl.when(t < half)
    def _():
        for copy in third_edges:
            copy.start()

    lane = lax.broadcasted_iota(jnp.int32, (8, LANES), 1)
    low_edge = lane == 0
    high_edge = lane == LANES - 1
    full = range(BASE, BASE + 2 * HALO + rows, 8)
    inner = range(BASE + 8, BASE + 2 * HALO + rows - 8, 8)
    strip = range(BASE + HALO, BASE + HALO + rows, 8)

    def half_step(state, kind, step, chunks):
        for row in chunks:
            values, _ = advanced(state, drags.at[kind], row, 0.5 * step, 1.0, low_edge, high_edge)
            for field in range(3):
                for side in (0, 1):
                    mid[field, side, pl.ds(row, 8), :] = values[field][side]

    def end_step(state, kind, step, chunks, put):
        for row in chunks:
            values, _ = advanced(mid, drags.at[kind + 1], row, 0.5 * step, 0.5, low_edge, high_edge)
            for field in range(3):
                for side in (0, 1):
                    put(field, side, row, values[field][side] + 0.5 * state[field, side, pl.ds(row, 8), :])

    def heun(state, kind, step, chunks, put):
        half_step(state, kind, step, chunks)
        end_step(state, kind, step, chunks if put is not None else chunks, put)

    def fine_steps(state, count, chunks):
        def put(field, side, row, value):
            state[field, side, pl.ds(row, 8), :] = value

        def step(_, carry):
            heun(state, 0, time_step, chunks, put)
            return carry

        lax.fori_loop(0, count, step, 0)

    for copy in first_edges + drag_edges:
        copy.wait()
    for row in full:
        for side in (0, 1):
            base = 2.0 * drag_raw[0, side, pl.ds(row, 8), :] + 4.0
            for kind, step in ((0, time_step), (2, coarse_step)):
                drags[kind, side, pl.ds(row, 8), :] = 1.0 - (0.5 * step) * base
                drags[kind + 1, side, pl.ds(row, 8), :] = 0.5 - (0.25 * step) * base

    fine_steps(first, STEPS - 4, full)
    fine_steps(first, 4, inner)

    is_first = t == times - 2
    for field in range(3):
        for side in (0, 1):
            second[field, side, own, :] = jnp.where(
                is_first, init_ref[field, :, side * LANES : (side + 1) * LANES], first[field, side, own, :]
            )
    second_edges = edges_of(second, second_send, second_recv)
    for copy in second_edges:
        copy.start()
    for copy in second_edges:
        copy.wait_recv()

    half_step(second, 2, coarse_step, inner)

    def put_gain(field, side, row, value):
        gained[field, side, pl.ds(row - BASE - HALO, 8), :] = value

    end_step(second, 2, coarse_step, strip, put_gain)
    for copy in second_edges:
        copy.wait_send()
    fine_steps(second, STEPS - 4, full)
    fine_steps(second, 4, inner)
    own_defect[...] = second[:, :, own, :] - gained[...]

    d_own = pl.ds(HALO, rows)

    def defect_copy(turn):
        target = slot_group * half + half - 1 - turn
        return remote(
            own_defect,
            defects.at[slot_place, :, :, d_own, :],
            defect_send.at[turn],
            defect_recv.at[slot_place],
            (target, z),
        )

    def send_defect(turn, carry):
        defect_copy(turn).start()
        return carry

    lax.fori_loop(0, half - slot_place, send_defect, 0)

    def edge_copies(turn):
        return (
            remote(
                defects.at[turn, :, :, pl.ds(rows, HALO), :],
                defects.at[turn, :, :, pl.ds(0, HALO), :],
                edge_send.at[0, turn], edge_recv.at[0, turn], (t, down),
            ),
            remote(
                defects.at[turn, :, :, pl.ds(HALO, HALO), :],
                defects.at[turn, :, :, pl.ds(HALO + rows, HALO), :],
                edge_send.at[1, turn], edge_recv.at[1, turn], (t, up),
            ),
        )

    def pass_edges(turn, carry):
        remote(
            own_defect, defects.at[turn, :, :, d_own, :], defect_send.at[turn], defect_recv.at[turn], (t, z)
        ).wait_recv()
        for copy in edge_copies(turn):
            copy.start()
        return carry

    ahead = jnp.minimum(jnp.where(t < half, LOOK, half), place + 1)
    lax.fori_loop(0, ahead, pass_edges, 0)

    @pl.when(t >= half)
    def _():
        remote(coarse_end, third.at[:, :, own, :], init_send.at[0], own_recv, (t, z)).wait_recv()

    for copy in third_edges:
        copy.wait_recv()

    def coarse(turn, chunks):
        for copy in edge_copies(turn):
            copy.wait_recv()

        def put(field, side, row, value):
            third[field, side, pl.ds(row, 8), :] = value + defects[turn, field, side, pl.ds(row - BASE, 8), :]

        half_step(third, 2, coarse_step, chunks)
        end_step(third, 2, coarse_step, chunks, put)

    def chain(chunks):
        def step(turn, carry):
            @pl.when(turn + ahead <= place)
            def _():
                pass_edges(turn + ahead, 0)

            coarse(turn, chunks)
            return carry

        return step

    @pl.when(t < half)
    def _():
        for copy in third_edges:
            copy.wait_send()

    middle = jnp.minimum(place, half // 2)
    lax.fori_loop(0, middle, chain(full), 0)
    lax.fori_loop(middle, place, chain(inner), 0)

    fourth[:, :, own, :] = third[:, :, own, :]
    fourth_edges = edges_of(fourth, fourth_send, fourth_recv)
    for copy in fourth_edges:
        copy.start()

    for copy in edge_copies(place):
        copy.wait_recv()

    def put_end(field, side, row, value):
        value = value + defects[place, field, side, pl.ds(row - BASE, 8), :]
        coarse_end[field, side, pl.ds(row - BASE - HALO, 8), :] = value
        c_ref[0, field, pl.ds(row - BASE - HALO, 8), side * LANES : (side + 1) * LANES] = value

    half_step(third, 2, coarse_step, inner)
    end_step(third, 2, coarse_step, strip, put_end)

    def hand_copies(turn):
        target = times - 1 - turn
        return (
            remote(coarse_end, third.at[:, :, own, :], hand_send.at[0, turn], own_recv, (target, z)),
            remote(
                coarse_end.at[:, :, pl.ds(rows - HALO, HALO), :], third.at[:, :, upper, :],
                hand_send.at[1, turn], start_recv.at[0], (target, down),
            ),
            remote(
                coarse_end.at[:, :, pl.ds(0, HALO), :], third.at[:, :, lower, :],
                hand_send.at[2, turn], start_recv.at[1], (target, up),
            ),
        )

    @pl.when(t == half - 1)
    def _():
        def hand(turn, carry):
            for copy in hand_copies(turn):
                copy.start()
            return carry

        lax.fori_loop(0, half, hand, 0)

    for copy in fourth_edges:
        copy.wait()
    fine_steps(fourth, STEPS - 5, full)
    fine_steps(fourth, 4, inner)
    for field in range(3):
        for side in (0, 1):
            f_ref[0, field, :, side * LANES : (side + 1) * LANES] = fourth[field, side, own, :]

    def sent_defect(turn, carry):
        defect_copy(turn).wait_send()
        return carry

    lax.fori_loop(0, half - slot_place, sent_defect, 0)

    def sent_edges(turn, carry):
        for copy in edge_copies(turn):
            copy.wait_send()
        return carry

    lax.fori_loop(0, place + 1, sent_edges, 0)

    @pl.when(t == half - 1)
    def _():
        def handed(turn, carry):
            for copy in hand_copies(turn):
                copy.wait_send()
            return carry

        lax.fori_loop(0, half, handed, 0)


def solution(mesh):
    times, strips = mesh.shape["tm"], mesh.shape["space"]
    half = times // 2

    def body(initial_state, c_guess, friction):
        rows = friction.shape[0]
        tall = BASE + 2 * HALO + rows + 8
        state = pltpu.VMEM((3, 2, tall, LANES), jnp.float32)
        part = pltpu.VMEM((3, 2, rows, LANES), jnp.float32)
        dma = pltpu.SemaphoreType.DMA
        vmem = pl.BlockSpec(memory_space=pltpu.VMEM)
        shape = jax.ShapeDtypeStruct(c_guess.shape, jnp.float32)
        return pl.pallas_call(
            functools.partial(kernel, times, strips, rows),
            out_shape=(shape, shape),
            in_specs=[vmem] * 3,
            out_specs=(vmem, vmem),
            scratch_shapes=[
                state, state, state, state, state,
                pltpu.VMEM((1, 2, tall, LANES), jnp.float32),
                pltpu.VMEM((4, 2, tall, LANES), jnp.float32),
                part,
                pltpu.VMEM((half, 3, 2, 2 * HALO + rows, LANES), jnp.float32),
                part,
                part,
                dma((2,)), dma((2,)), dma((2,)), dma((2,)), dma((2,)), dma((2,)), dma,
                dma((2,)), dma((2,)), dma((half,)), dma((half,)), dma((2, half)), dma((2, half)),
                dma((3, half)), dma((2,)), dma((2,)),
            ],
            compiler_params=pltpu.CompilerParams(collective_id=0, has_side_effects=True),
            cost_estimate=pl.CostEstimate(flops=100_000_000, bytes_accessed=1_000_000, transcendentals=0),
        )(initial_state, c_guess, friction)

    return jax.shard_map(
        body,
        mesh=mesh,
        in_specs=(P(None, "space", None), P("tm", None, "space", None), P("space", None)),
        out_specs=(P("tm", None, "space", None), P("tm", None, "space", None)),
        check_vma=False,
    )
```

time: 198 us -> 64.4 us (0.33)
  the two profiles are of different devices: /device:TPU:24 before, /device:TPU:18 now
where the time goes in v1:
time: 64.4 us; the launch traced here: 64.2 us
  Pallas kernels  61.3 us (95%)
  local copies, waits for them, and re-layouts  2.19 us (3%)
  between operations  0.65 us (1%)
    pallas_call x1, Pallas kernels, body(): pl.pallas_call(functools.partial(kernel, times, strips, rows), out_shape=...  61.3 us
    unnamed x4, local copies, waits for them, and re-layouts  2.19 us

profile of v1, /device:TPU:18, one launch (start us, length us, event | category | flops | bytes accessed | tf_op | source)
XLA Modules:
  0.0 64.2 jit_solution(7669833630570953670)
XLA Ops:
  0.6 61.3 %shard_map.50 = (f32[1,3,24,256]{3,2,1,0:T(8,128)}, f32[1,3,24,256]{3,2,1,0:T(8,128)}) custom-call(f32[3,24,256]{2,1,0:T(8,128)} %init_ref.1, f32[1,3,24,256]{3,2,1,0:T(8,128)} %guess_ref.1, f32[24,256]{1,0:T(8,128)} %fric_ref.1), custom_call_target="tpu_custom_call" | custom-call | flops 100000000 | bytes 1000000 | tf_op jit(solution)/shard_map/pallas_call | solution.py:380
  62.0 0.0 copy-start
  62.0 1.6 %copy.7 = f32[1,3,24,256]{3,2,1,0:T(8,128)} copy(f32[1,3,24,256]{3,2,1,0:T(8,128)} %get-tuple-element.4) | data formatting | bytes 147456
  63.5 0.0 copy-done
  63.5 0.6 copy.8
Async XLA Ops:
  62.0 1.6 %copy-start = (f32[1,3,24,256]{3,2,1,0:T(8,128)S(1)}, f32[1,3,24,256]{3,2,1,0:T(8,128)}, u32[]{:S(2)}) copy-start(f32[1,3,24,256]{3,2,1,0:T(8,128)} %get-tuple-element.5) | copy-start | bytes 221188

commit v2 on v1

--- a/solution.py
+++ b/solution.py
@@ -62,21 +62,17 @@
 def kernel(
     times, strips, rows,
     init_ref, guess_ref, fric_ref, c_ref, f_ref,
-    first, second, third, fourth, mid, drag_raw, drags, gained, defects, own_defect, coarse_end,
-    halo_send, halo_recv, fric_send, fric_recv, init_send, start_recv, own_recv,
+    first, second, third, fourth, mid, drag_raw, drags, gained, defects, own_defect,
+    halo_send, halo_recv, fric_send, fric_recv, init_send, start_recv,
     second_send, second_recv, defect_send, defect_recv, edge_send, edge_recv,
-    hand_send, fourth_send, fourth_recv,
+    fourth_send, fourth_recv,
 ):
     half = times // 2
     t = lax.axis_index("tm")
     z = lax.axis_index("space")
     up = lax.rem(z + strips - 1, strips)
     down = lax.rem(z + 1, strips)
-    group = t // half
-    place = lax.rem(t, half)
     slot = lax.rem(t + 2, times)
-    slot_group = slot // half
-    slot_place = lax.rem(slot, half)
 
     own = pl.ds(BASE + HALO, rows)
     upper = pl.ds(BASE, HALO)
@@ -105,17 +101,6 @@
     for other in range(1, times):
         greet(lax.rem(t + other, times), z)
 
-    @pl.when(t == half - 1)
-    def _():
-        for later in range(half, times):
-            greet(later, up)
-            greet(later, down)
-
-    @pl.when(t >= half)
-    def _():
-        greet(half - 1, up)
-        greet(half - 1, down)
-
     is_last = t == times - 1
     for field in range(3):
         for side in (0, 1):
@@ -124,25 +109,18 @@
     for side in (0, 1):
         drag_raw[0, side, own, :] = fric_ref[:, side * LANES : (side + 1) * LANES]
 
-    @pl.when(t < half)
-    def _():
-        for field in range(3):
-            for side in (0, 1):
-                third[field, side, own, :] = init_ref[field, :, side * LANES : (side + 1) * LANES]
-
-    greeted = jnp.where(t == half - 1, 2 * half, jnp.where(t >= half, 2, 0))
-    pl.semaphore_wait(barrier, times + 1 + greeted)
+    for field in range(3):
+        for side in (0, 1):
+            third[0, field, side, own, :] = init_ref[field, :, side * LANES : (side + 1) * LANES]
+
+    pl.semaphore_wait(barrier, times + 1)
 
     first_edges = edges_of(first, halo_send, halo_recv)
     drag_edges = edges_of(drag_raw, fric_send, fric_recv)
-    third_edges = edges_of(third, init_send, start_recv)
-    for copy in first_edges + drag_edges:
+    third_edges = edges_of(third.at[0], init_send.at[0], start_recv.at[0])
+    later_edges = edges_of(third.at[1], init_send.at[1], start_recv.at[1])
+    for copy in first_edges + drag_edges + third_edges:
         copy.start()
-
-    @pl.when(t < half)
-    def _():
-        for copy in third_edges:
-            copy.start()
 
     lane = lax.broadcasted_iota(jnp.int32, (8, LANES), 1)
     low_edge = lane == 0
@@ -218,121 +196,115 @@
     d_own = pl.ds(HALO, rows)
 
     def defect_copy(turn):
-        target = slot_group * half + half - 1 - turn
+        target = times - 1 - turn
         return remote(
-            own_defect,
-            defects.at[slot_place, :, :, d_own, :],
-            defect_send.at[turn],
-            defect_recv.at[slot_place],
-            (target, z),
-        )
-
-    def send_defect(turn, carry):
-        defect_copy(turn).start()
+            own_defect, defects.at[slot, :, :, d_own, :], defect_send.at[turn], defect_recv.at[slot], (target, z)
+        )
+
+    def each_defect(act):
+        def one(turn, carry):
+            @pl.when(times - 1 - turn != t)
+            def _():
+                act(defect_copy(turn))
+
+            return carry
+
+        lax.fori_loop(0, times - slot, one, 0)
+
+    each_defect(lambda copy: copy.start())
+
+    @pl.when(t >= times - 2)
+    def _():
+        defects[slot, :, :, d_own, :] = own_defect[...]
+
+    def each_edge(turn, act):
+        need = 2 * (half - 1 - lax.rem(turn, half))
+
+        def copies(count):
+            return (
+                remote(
+                    defects.at[turn, :, :, pl.ds(HALO + rows - count, count), :],
+                    defects.at[turn, :, :, pl.ds(HALO - count, count), :],
+                    edge_send.at[0, turn], edge_recv.at[0, turn], (t, down),
+                ),
+                remote(
+                    defects.at[turn, :, :, pl.ds(HALO, count), :],
+                    defects.at[turn, :, :, pl.ds(HALO + rows, count), :],
+                    edge_send.at[1, turn], edge_recv.at[1, turn], (t, up),
+                ),
+            )
+
+        @pl.when(need > 8)
+        def _():
+            for copy in copies(16):
+                act(copy)
+
+        @pl.when((need > 0) & (need <= 8))
+        def _():
+            for copy in copies(8):
+                act(copy)
+
+    def pass_edges(turn, carry):
+        @pl.when(turn != slot)
+        def _():
+            remote(
+                own_defect, defects.at[turn, :, :, d_own, :], defect_send.at[turn], defect_recv.at[turn], (t, z)
+            ).wait_recv()
+
+        each_edge(turn, lambda copy: copy.start())
         return carry
 
-    lax.fori_loop(0, half - slot_place, send_defect, 0)
-
-    def edge_copies(turn):
-        return (
-            remote(
-                defects.at[turn, :, :, pl.ds(rows, HALO), :],
-                defects.at[turn, :, :, pl.ds(0, HALO), :],
-                edge_send.at[0, turn], edge_recv.at[0, turn], (t, down),
-            ),
-            remote(
-                defects.at[turn, :, :, pl.ds(HALO, HALO), :],
-                defects.at[turn, :, :, pl.ds(HALO + rows, HALO), :],
-                edge_send.at[1, turn], edge_recv.at[1, turn], (t, up),
-            ),
-        )
-
-    def pass_edges(turn, carry):
-        remote(
-            own_defect, defects.at[turn, :, :, d_own, :], defect_send.at[turn], defect_recv.at[turn], (t, z)
-        ).wait_recv()
-        for copy in edge_copies(turn):
-            copy.start()
-        return carry
-
-    ahead = jnp.minimum(jnp.where(t < half, LOOK, half), place + 1)
+    ahead = jnp.minimum(LOOK, t + 1)
     lax.fori_loop(0, ahead, pass_edges, 0)
+
+    for copy in third_edges:
+        copy.wait()
+
+    def chain(state, chunks):
+        def step(turn, carry):
+            @pl.when(turn + ahead <= t)
+            def _():
+                pass_edges(turn + ahead, 0)
+
+            half_step(state, 2, coarse_step, chunks)
+            each_edge(turn, lambda copy: copy.wait_recv())
+
+            def put(field, side, row, value):
+                state[field, side, pl.ds(row, 8), :] = value + defects[turn, field, side, pl.ds(row - BASE, 8), :]
+
+            end_step(state, 2, coarse_step, chunks, put)
+            return carry
+
+        return step
+
+    wide = max(half - 4, 0)
+    lax.fori_loop(0, jnp.minimum(t, wide), chain(third.at[0], full), 0)
+    lax.fori_loop(wide, jnp.minimum(t, half), chain(third.at[0], inner), 0)
 
     @pl.when(t >= half)
     def _():
-        remote(coarse_end, third.at[:, :, own, :], init_send.at[0], own_recv, (t, z)).wait_recv()
-
-    for copy in third_edges:
-        copy.wait_recv()
-
-    def coarse(turn, chunks):
-        for copy in edge_copies(turn):
-            copy.wait_recv()
-
-        def put(field, side, row, value):
-            third[field, side, pl.ds(row, 8), :] = value + defects[turn, field, side, pl.ds(row - BASE, 8), :]
-
-        half_step(third, 2, coarse_step, chunks)
-        end_step(third, 2, coarse_step, chunks, put)
-
-    def chain(chunks):
-        def step(turn, carry):
-            @pl.when(turn + ahead <= place)
-            def _():
-                pass_edges(turn + ahead, 0)
-
-            coarse(turn, chunks)
-            return carry
-
-        return step
-
-    @pl.when(t < half)
-    def _():
-        for copy in third_edges:
-            copy.wait_send()
-
-    middle = jnp.minimum(place, half // 2)
-    lax.fori_loop(0, middle, chain(full), 0)
-    lax.fori_loop(middle, place, chain(inner), 0)
-
-    fourth[:, :, own, :] = third[:, :, own, :]
+        third[1, :, :, own, :] = third[0, :, :, own, :]
+        for copy in later_edges:
+            copy.start()
+        for copy in later_edges:
+            copy.wait()
+        lax.fori_loop(half, jnp.minimum(t, half + wide), chain(third.at[1], full), 0)
+        lax.fori_loop(half + wide, t, chain(third.at[1], inner), 0)
+
+    state = third.at[t // half]
+    fourth[:, :, own, :] = state[:, :, own, :]
     fourth_edges = edges_of(fourth, fourth_send, fourth_recv)
     for copy in fourth_edges:
         copy.start()
 
-    for copy in edge_copies(place):
-        copy.wait_recv()
-
     def put_end(field, side, row, value):
-        value = value + defects[place, field, side, pl.ds(row - BASE, 8), :]
-        coarse_end[field, side, pl.ds(row - BASE - HALO, 8), :] = value
-        c_ref[0, field, pl.ds(row - BASE - HALO, 8), side * LANES : (side + 1) * LANES] = value
-
-    half_step(third, 2, coarse_step, inner)
-    end_step(third, 2, coarse_step, strip, put_end)
-
-    def hand_copies(turn):
-        target = times - 1 - turn
-        return (
-            remote(coarse_end, third.at[:, :, own, :], hand_send.at[0, turn], own_recv, (target, z)),
-            remote(
-                coarse_end.at[:, :, pl.ds(rows - HALO, HALO), :], third.at[:, :, upper, :],
-                hand_send.at[1, turn], start_recv.at[0], (target, down),
-            ),
-            remote(
-                coarse_end.at[:, :, pl.ds(0, HALO), :], third.at[:, :, lower, :],
-                hand_send.at[2, turn], start_recv.at[1], (target, up),
-            ),
-        )
-
-    @pl.when(t == half - 1)
-    def _():
-        def hand(turn, carry):
-            for copy in hand_copies(turn):
-                copy.start()
-            return carry
-
-        lax.fori_loop(0, half, hand, 0)
+        c_ref[0, field, pl.ds(row - BASE - HALO, 8), side * LANES : (side + 1) * LANES] = (
+            value + defects[t, field, side, pl.ds(row - BASE, 8), :]
+        )
+
+    half_step(state, 2, coarse_step, inner)
+    each_edge(t, lambda copy: copy.wait_recv())
+    end_step(state, 2, coarse_step, strip, put_end)
 
     for copy in fourth_edges:
         copy.wait()
@@ -342,32 +314,17 @@
         for side in (0, 1):
             f_ref[0, field, :, side * LANES : (side + 1) * LANES] = fourth[field, side, own, :]
 
-    def sent_defect(turn, carry):
-        defect_copy(turn).wait_send()
+    each_defect(lambda copy: copy.wait_send())
+
+    def sent_edges(turn, carry):
+        each_edge(turn, lambda copy: copy.wait_send())
         return carry
 
-    lax.fori_loop(0, half - slot_place, sent_defect, 0)
-
-    def sent_edges(turn, carry):
-        for copy in edge_copies(turn):
-            copy.wait_send()
-        return carry
-
-    lax.fori_loop(0, place + 1, sent_edges, 0)
-
-    @pl.when(t == half - 1)
-    def _():
-        def handed(turn, carry):
-            for copy in hand_copies(turn):
-                copy.wait_send()
-            return carry
-
-        lax.fori_loop(0, half, handed, 0)
+    lax.fori_loop(0, t + 1, sent_edges, 0)
 
 
 def solution(mesh):
     times, strips = mesh.shape["tm"], mesh.shape["space"]
-    half = times // 2
 
     def body(initial_state, c_guess, friction):
         rows = friction.shape[0]
@@ -376,23 +333,24 @@
         part = pltpu.VMEM((3, 2, rows, LANES), jnp.float32)
         dma = pltpu.SemaphoreType.DMA
         vmem = pl.BlockSpec(memory_space=pltpu.VMEM)
-        shape = jax.ShapeDtypeStruct(c_guess.shape, jnp.float32)
+        shape = pltpu.VMEM(c_guess.shape, jnp.float32)
         return pl.pallas_call(
             functools.partial(kernel, times, strips, rows),
             out_shape=(shape, shape),
             in_specs=[vmem] * 3,
             out_specs=(vmem, vmem),
             scratch_shapes=[
-                state, state, state, state, state,
+                state, state,
+                pltpu.VMEM((2, 3, 2, tall, LANES), jnp.float32),
+                state, state,
                 pltpu.VMEM((1, 2, tall, LANES), jnp.float32),
                 pltpu.VMEM((4, 2, tall, LANES), jnp.float32),
                 part,
-                pltpu.VMEM((half, 3, 2, 2 * HALO + rows, LANES), jnp.float32),
+                pltpu.VMEM((times, 3, 2, 2 * HALO + rows, LANES), jnp.float32),
                 part,
-                part,
-                dma((2,)), dma((2,)), dma((2,)), dma((2,)), dma((2,)), dma((2,)), dma,
-                dma((2,)), dma((2,)), dma((half,)), dma((half,)), dma((2, half)), dma((2, half)),
-                dma((3, half)), dma((2,)), dma((2,)),
+                dma((2,)), dma((2,)), dma((2,)), dma((2,)), dma((2, 2)), dma((2, 2)),
+                dma((2,)), dma((2,)), dma((times,)), dma((times,)), dma((2, times)), dma((2, times)),
+                dma((2,)), dma((2,)),
             ],
             compiler_params=pltpu.CompilerParams(collective_id=0, has_side_effects=True),
             cost_estimate=pl.CostEstimate(flops=100_000_000, bytes_accessed=1_000_000, transcendentals=0),

time: 64.4 us -> 61.4 us (0.953)
  the two profiles are of different devices: /device:TPU:18 before, /device:TPU:24 now
where the time goes in v2:
time: 61.4 us; the launch traced here: 61.3 us
  Pallas kernels  59.4 us (97%)
  local copies, waits for them, and re-layouts  1.27 us (2%)
  between operations  0.64 us (1%)
    pallas_call x1, Pallas kernels, body(): pl.pallas_call(functools.partial(kernel, times, strips, rows), out_shape=...  59.4 us
    unnamed x2, local copies, waits for them, and re-layouts  1.27 us

profile of v2, /device:TPU:24, one launch (start us, length us, event | category | flops | bytes accessed | tf_op | source)
XLA Modules:
  0.0 61.3 jit_solution(11145436580821418393)
XLA Ops:
  0.6 59.4 %shard_map.50 = (f32[1,3,24,256]{3,2,1,0:T(8,128)S(1)}, f32[1,3,24,256]{3,2,1,0:T(8,128)S(1)}) custom-call(f32[3,24,256]{2,1,0:T(8,128)} %init_ref.1, f32[1,3,24,256]{3,2,1,0:T(8,128)} %guess_ref.1, f32[24,256]{1,0:T(8,128)} %fric_ref.1), custom_call_target="tpu_custom_call" | custom-call | flops 100000000 | bytes 1000000 | tf_op jit(solution)/shard_map/pallas_call | solution.py:337
  60.0 0.6 %copy.7 = f32[1,3,24,256]{3,2,1,0:T(8,128)} copy(f32[1,3,24,256]{3,2,1,0:T(8,128)S(1)} %get-tuple-element.2) | data formatting | bytes 147456
  60.6 0.6 %copy.8 = f32[1,3,24,256]{3,2,1,0:T(8,128)} copy(f32[1,3,24,256]{3,2,1,0:T(8,128)S(1)} %get-tuple-element.3) | data formatting | bytes 147456

commit v3 on v2

--- a/solution.py
+++ b/solution.py
@@ -1,4 +1,5 @@
 import functools
+import math
 
 import jax
 import jax.numpy as jnp
@@ -15,7 +16,6 @@
 HALO = 16
 LANES = 128
 BASE = 8
-LOOK = 3
 
 
 def shifted_lanes(pair, by, edge):
@@ -65,14 +65,22 @@
     first, second, third, fourth, mid, drag_raw, drags, gained, defects, own_defect,
     halo_send, halo_recv, fric_send, fric_recv, init_send, start_recv,
     second_send, second_recv, defect_send, defect_recv, edge_send, edge_recv,
-    fourth_send, fourth_recv,
+    fourth_send, fourth_recv, hand_send, hand_recv,
 ):
     half = times // 2
+    span = math.isqrt(times)
     t = lax.axis_index("tm")
     z = lax.axis_index("space")
     up = lax.rem(z + strips - 1, strips)
     down = lax.rem(z + 1, strips)
+    place = lax.rem(t, half)
     slot = lax.rem(t + 2, times)
+    slot_place = lax.rem(slot, half)
+    hands = (t >= half - span) & (t < half)
+    last = jnp.where(hands, half - 1, place)
+    slot_end = slot // half * half + half
+    slot_low = jnp.where(slot < half, jnp.minimum(slot, half - span), slot)
+    handed = half // span
 
     own = pl.ds(BASE + HALO, rows)
     upper = pl.ds(BASE, HALO)
@@ -100,6 +108,18 @@
     greet(t, down)
     for other in range(1, times):
         greet(lax.rem(t + other, times), z)
+
+    @pl.when(hands)
+    def _():
+        for turn in range(1, handed + 1):
+            greet(t + turn * span, up)
+            greet(t + turn * span, down)
+
+    @pl.when(t >= half)
+    def _():
+        giver = half - span + lax.rem(t, span)
+        greet(giver, up)
+        greet(giver, down)
 
     is_last = t == times - 1
     for field in range(3):
@@ -109,18 +129,25 @@
     for side in (0, 1):
         drag_raw[0, side, own, :] = fric_ref[:, side * LANES : (side + 1) * LANES]
 
-    for field in range(3):
-        for side in (0, 1):
-            third[0, field, side, own, :] = init_ref[field, :, side * LANES : (side + 1) * LANES]
-
-    pl.semaphore_wait(barrier, times + 1)
+    @pl.when(t < half)
+    def _():
+        for field in range(3):
+            for part in (0, 1):
+                third[field, part, own, :] = init_ref[field, :, part * LANES : (part + 1) * LANES]
+
+    greeted = jnp.where(hands, 2 * handed, jnp.where(t >= half, 2, 0))
+    pl.semaphore_wait(barrier, times + 1 + greeted)
 
     first_edges = edges_of(first, halo_send, halo_recv)
     drag_edges = edges_of(drag_raw, fric_send, fric_recv)
-    third_edges = edges_of(third.at[0], init_send.at[0], start_recv.at[0])
-    later_edges = edges_of(third.at[1], init_send.at[1], start_recv.at[1])
-    for copy in first_edges + drag_edges + third_edges:
+    third_edges = edges_of(third, init_send, start_recv)
+    for copy in first_edges + drag_edges:
         copy.start()
+
+    @pl.when(t < half)
+    def _():
+        for copy in third_edges:
+            copy.start()
 
     lane = lax.broadcasted_iota(jnp.int32, (8, LANES), 1)
     low_edge = lane == 0
@@ -195,30 +222,32 @@
 
     d_own = pl.ds(HALO, rows)
 
-    def defect_copy(turn):
-        target = times - 1 - turn
-        return remote(
-            own_defect, defects.at[slot, :, :, d_own, :], defect_send.at[turn], defect_recv.at[slot], (target, z)
-        )
-
     def each_defect(act):
         def one(turn, carry):
-            @pl.when(times - 1 - turn != t)
+            target = slot_end - 1 - turn
+
+            @pl.when(target != t)
             def _():
-                act(defect_copy(turn))
+                act(
+                    remote(
+                        own_defect, defects.at[slot_place, :, :, d_own, :],
+                        defect_send.at[turn], defect_recv.at[slot_place], (target, z),
+                    )
+                )
 
             return carry
 
-        lax.fori_loop(0, times - slot, one, 0)
+        lax.fori_loop(0, slot_end - slot_low, one, 0)
 
     each_defect(lambda copy: copy.start())
-
-    @pl.when(t >= times - 2)
-    def _():
-        defects[slot, :, :, d_own, :] = own_defect[...]
+    keeps = (t >= slot_low) & (t < slot_end)
+
+    @pl.when(keeps)
+    def _():
+        defects[slot_place, :, :, d_own, :] = own_defect[...]
 
     def each_edge(turn, act):
-        need = 2 * (half - 1 - lax.rem(turn, half))
+        need = 2 * (half - 1 - turn)
 
         def copies(count):
             return (
@@ -245,7 +274,7 @@
                 act(copy)
 
     def pass_edges(turn, carry):
-        @pl.when(turn != slot)
+        @pl.when(jnp.logical_not(keeps & (turn == slot_place)))
         def _():
             remote(
                 own_defect, defects.at[turn, :, :, d_own, :], defect_send.at[turn], defect_recv.at[turn], (t, z)
@@ -254,57 +283,74 @@
         each_edge(turn, lambda copy: copy.start())
         return carry
 
-    ahead = jnp.minimum(LOOK, t + 1)
-    lax.fori_loop(0, ahead, pass_edges, 0)
+    lax.fori_loop(0, last + 1, pass_edges, 0)
+
+    @pl.when(t < half)
+    def _():
+        for copy in third_edges:
+            copy.wait_send()
+
+    @pl.when(t >= half)
+    def _():
+        remote(third.at[:, :, own, :], third.at[:, :, own, :], hand_send.at[0, 0], hand_recv, (t, z)).wait_recv()
 
     for copy in third_edges:
-        copy.wait()
-
-    def chain(state, chunks):
+        copy.wait_recv()
+
+    def chain(chunks):
         def step(turn, carry):
-            @pl.when(turn + ahead <= t)
-            def _():
-                pass_edges(turn + ahead, 0)
-
-            half_step(state, 2, coarse_step, chunks)
+            half_step(third, 2, coarse_step, chunks)
             each_edge(turn, lambda copy: copy.wait_recv())
 
-            def put(field, side, row, value):
-                state[field, side, pl.ds(row, 8), :] = value + defects[turn, field, side, pl.ds(row - BASE, 8), :]
-
-            end_step(state, 2, coarse_step, chunks, put)
+            def put(field, part, row, value):
+                third[field, part, pl.ds(row, 8), :] = value + defects[turn, field, part, pl.ds(row - BASE, 8), :]
+
+            end_step(third, 2, coarse_step, chunks, put)
             return carry
 
         return step
 
     wide = max(half - 4, 0)
-    lax.fori_loop(0, jnp.minimum(t, wide), chain(third.at[0], full), 0)
-    lax.fori_loop(wide, jnp.minimum(t, half), chain(third.at[0], inner), 0)
-
-    @pl.when(t >= half)
-    def _():
-        third[1, :, :, own, :] = third[0, :, :, own, :]
-        for copy in later_edges:
-            copy.start()
-        for copy in later_edges:
-            copy.wait()
-        lax.fori_loop(half, jnp.minimum(t, half + wide), chain(third.at[1], full), 0)
-        lax.fori_loop(half + wide, t, chain(third.at[1], inner), 0)
-
-    state = third.at[t // half]
-    fourth[:, :, own, :] = state[:, :, own, :]
+    lax.fori_loop(0, jnp.minimum(place, wide), chain(full), 0)
+    lax.fori_loop(wide, place, chain(inner), 0)
+
+    fourth[:, :, own, :] = third[:, :, own, :]
     fourth_edges = edges_of(fourth, fourth_send, fourth_recv)
     for copy in fourth_edges:
         copy.start()
 
-    def put_end(field, side, row, value):
-        c_ref[0, field, pl.ds(row - BASE - HALO, 8), side * LANES : (side + 1) * LANES] = (
-            value + defects[t, field, side, pl.ds(row - BASE, 8), :]
-        )
-
-    half_step(state, 2, coarse_step, inner)
-    each_edge(t, lambda copy: copy.wait_recv())
-    end_step(state, 2, coarse_step, strip, put_end)
+    def put_out():
+        for field in range(3):
+            for part in (0, 1):
+                c_ref[0, field, :, part * LANES : (part + 1) * LANES] = third[field, part, own, :]
+
+    chain(inner)(place, 0)
+    put_out()
+    lax.fori_loop(place + 1, last + 1, chain(inner), 0)
+
+    def each_hand(act):
+        def one(turn, carry):
+            target = t + span * turn + span
+            act(remote(third.at[:, :, own, :], third.at[:, :, own, :], hand_send.at[0, turn], hand_recv, (target, z)))
+            act(
+                remote(
+                    third.at[:, :, own_last, :], third.at[:, :, upper, :],
+                    hand_send.at[1, turn], start_recv.at[0], (target, down),
+                )
+            )
+            act(
+                remote(
+                    third.at[:, :, own_first, :], third.at[:, :, lower, :],
+                    hand_send.at[2, turn], start_recv.at[1], (target, up),
+                )
+            )
+            return carry
+
+        lax.fori_loop(0, handed, one, 0)
+
+    @pl.when(hands)
+    def _():
+        each_hand(lambda copy: copy.start())
 
     for copy in fourth_edges:
         copy.wait()
@@ -320,7 +366,11 @@
         each_edge(turn, lambda copy: copy.wait_send())
         return carry
 
-    lax.fori_loop(0, t + 1, sent_edges, 0)
+    lax.fori_loop(0, last + 1, sent_edges, 0)
+
+    @pl.when(hands)
+    def _():
+        each_hand(lambda copy: copy.wait_send())
 
 
 def solution(mesh):
@@ -341,16 +391,15 @@
             out_specs=(vmem, vmem),
             scratch_shapes=[
                 state, state,
-                pltpu.VMEM((2, 3, 2, tall, LANES), jnp.float32),
-                state, state,
+                state, state, state,
                 pltpu.VMEM((1, 2, tall, LANES), jnp.float32),
                 pltpu.VMEM((4, 2, tall, LANES), jnp.float32),
                 part,
-                pltpu.VMEM((times, 3, 2, 2 * HALO + rows, LANES), jnp.float32),
+                pltpu.VMEM((times // 2, 3, 2, 2 * HALO + rows, LANES), jnp.float32),
                 part,
-                dma((2,)), dma((2,)), dma((2,)), dma((2,)), dma((2, 2)), dma((2, 2)),
+                dma((2,)), dma((2,)), dma((2,)), dma((2,)), dma((2,)), dma((2,)),
                 dma((2,)), dma((2,)), dma((times,)), dma((times,)), dma((2, times)), dma((2, times)),
-                dma((2,)), dma((2,)),
+                dma((2,)), dma((2,)), dma((3, 4)), dma,
             ],
             compiler_params=pltpu.CompilerParams(collective_id=0, has_side_effects=True),
             cost_estimate=pl.CostEstimate(flops=100_000_000, bytes_accessed=1_000_000, transcendentals=0),

time: 61.4 us -> 52.6 us (0.86)
  Pallas kernels: 59.4 us -> 50.5 us
    pallas_call x1, Pallas kernels: 59.4 us -> 50.5 us  [body(): pl.pallas_call(functools.partial(kernel, times, strips, rows), out_shape=...]
where the time goes in v3:
time: 52.6 us; the launch traced here: 52.4 us
  Pallas kernels  50.5 us (96%)
  local copies, waits for them, and re-layouts  1.27 us (2%)
  between operations  0.64 us (1%)
    pallas_call x1, Pallas kernels, body(): pl.pallas_call(functools.partial(kernel, times, strips, rows), out_shape=...  50.5 us
    unnamed x2, local copies, waits for them, and re-layouts  1.27 us

profile of v3, /device:TPU:24, one launch (start us, length us, event | category | flops | bytes accessed | tf_op | source)
XLA Modules:
  0.0 52.4 jit_solution(3444491643589633680)
XLA Ops:
  0.6 50.5 %shard_map.50 = (f32[1,3,24,256]{3,2,1,0:T(8,128)S(1)}, f32[1,3,24,256]{3,2,1,0:T(8,128)S(1)}) custom-call(f32[3,24,256]{2,1,0:T(8,128)} %init_ref.1, f32[1,3,24,256]{3,2,1,0:T(8,128)} %guess_ref.1, f32[24,256]{1,0:T(8,128)} %fric_ref.1), custom_call_target="tpu_custom_call" | custom-call | flops 100000000 | bytes 1000000 | tf_op jit(solution)/shard_map/pallas_call | solution.py:387
  51.1 0.6 %copy.7 = f32[1,3,24,256]{3,2,1,0:T(8,128)} copy(f32[1,3,24,256]{3,2,1,0:T(8,128)S(1)} %get-tuple-element.2) | data formatting | bytes 147456
  51.8 0.6 %copy.8 = f32[1,3,24,256]{3,2,1,0:T(8,128)} copy(f32[1,3,24,256]{3,2,1,0:T(8,128)S(1)} %get-tuple-element.3) | data formatting | bytes 147456

commit v4 on v3

--- a/solution.py
+++ b/solution.py
@@ -65,7 +65,7 @@
     first, second, third, fourth, mid, drag_raw, drags, gained, defects, own_defect,
     halo_send, halo_recv, fric_send, fric_recv, init_send, start_recv,
     second_send, second_recv, defect_send, defect_recv, edge_send, edge_recv,
-    fourth_send, fourth_recv, hand_send, hand_recv,
+    fourth_send, fourth_recv, hand_send, hand_recv, share_send, met,
 ):
     half = times // 2
     span = math.isqrt(times)
@@ -106,20 +106,12 @@
 
     greet(t, up)
     greet(t, down)
-    for other in range(1, times):
-        greet(lax.rem(t + other, times), z)
-
-    @pl.when(hands)
-    def _():
-        for turn in range(1, handed + 1):
-            greet(t + turn * span, up)
-            greet(t + turn * span, down)
-
-    @pl.when(t >= half)
-    def _():
-        giver = half - span + lax.rem(t, span)
-        greet(giver, up)
-        greet(giver, down)
+    partners = []
+    for bit in range((times - 1).bit_length()):
+        far = 1 << bit
+        partners.append(t + far - 2 * far * lax.rem(t // far, 2))
+    for partner in partners:
+        greet(partner, z)
 
     is_last = t == times - 1
     for field in range(3):
@@ -135,9 +127,15 @@
             for part in (0, 1):
                 third[field, part, own, :] = init_ref[field, :, part * LANES : (part + 1) * LANES]
 
-    greeted = jnp.where(hands, 2 * handed, jnp.where(t >= half, 2, 0))
-    pl.semaphore_wait(barrier, times + 1 + greeted)
-
+    pl.semaphore_wait(barrier, 2 + len(partners))
+
+    def tell(turn):
+        pl.semaphore_signal(met.at[turn], inc=1, device_id=(partners[turn], z), device_id_type=MESH)
+
+    def hear(turn):
+        pl.semaphore_wait(met.at[turn], 1)
+
+    tell(0)
     first_edges = edges_of(first, halo_send, halo_recv)
     drag_edges = edges_of(drag_raw, fric_send, fric_recv)
     third_edges = edges_of(third, init_send, start_recv)
@@ -192,6 +190,10 @@
             for kind, step in ((0, time_step), (2, coarse_step)):
                 drags[kind, side, pl.ds(row, 8), :] = 1.0 - (0.5 * step) * base
                 drags[kind + 1, side, pl.ds(row, 8), :] = 0.5 - (0.25 * step) * base
+
+    hear(0)
+    if len(partners) > 1:
+        tell(1)
 
     fine_steps(first, STEPS - 4, full)
     fine_steps(first, 4, inner)
@@ -205,6 +207,10 @@
     second_edges = edges_of(second, second_send, second_recv)
     for copy in second_edges:
         copy.start()
+    if len(partners) > 1:
+        hear(1)
+    if len(partners) > 2:
+        tell(2)
     for copy in second_edges:
         copy.wait_recv()
 
@@ -214,12 +220,18 @@
         gained[field, side, pl.ds(row - BASE - HALO, 8), :] = value
 
     end_step(second, 2, coarse_step, strip, put_gain)
+    if len(partners) > 2:
+        hear(2)
+    if len(partners) > 3:
+        tell(3)
     for copy in second_edges:
         copy.wait_send()
     fine_steps(second, STEPS - 4, full)
     fine_steps(second, 4, inner)
     own_defect[...] = second[:, :, own, :] - gained[...]
 
+    if len(partners) > 3:
+        hear(3)
     d_own = pl.ds(HALO, rows)
 
     def each_defect(act):
@@ -285,6 +297,10 @@
 
     lax.fori_loop(0, last + 1, pass_edges, 0)
 
+    upper_core = lax.rem(z, 2) == 0
+    share_down = remote(third.at[:, :, own_last, :], third.at[:, :, upper, :], share_send, start_recv.at[0], (t, down))
+    share_up = remote(third.at[:, :, own_first, :], third.at[:, :, lower, :], share_send, start_recv.at[1], (t, up))
+
     @pl.when(t < half)
     def _():
         for copy in third_edges:
@@ -294,8 +310,24 @@
     def _():
         remote(third.at[:, :, own, :], third.at[:, :, own, :], hand_send.at[0, 0], hand_recv, (t, z)).wait_recv()
 
+        @pl.when(upper_core)
+        def _():
+            share_down.start()
+
+        @pl.when(jnp.logical_not(upper_core))
+        def _():
+            share_up.start()
+
     for copy in third_edges:
         copy.wait_recv()
+
+    @pl.when((t >= half) & upper_core)
+    def _():
+        share_down.wait_send()
+
+    @pl.when((t >= half) & jnp.logical_not(upper_core))
+    def _():
+        share_up.wait_send()
 
     def chain(chunks):
         def step(turn, carry):
@@ -332,18 +364,25 @@
         def one(turn, carry):
             target = t + span * turn + span
             act(remote(third.at[:, :, own, :], third.at[:, :, own, :], hand_send.at[0, turn], hand_recv, (target, z)))
-            act(
-                remote(
-                    third.at[:, :, own_last, :], third.at[:, :, upper, :],
-                    hand_send.at[1, turn], start_recv.at[0], (target, down),
+
+            @pl.when(upper_core)
+            def _():
+                act(
+                    remote(
+                        third.at[:, :, own_first, :], third.at[:, :, lower, :],
+                        hand_send.at[1, turn], start_recv.at[1], (target, up),
+                    )
                 )
-            )
-            act(
-                remote(
-                    third.at[:, :, own_first, :], third.at[:, :, lower, :],
-                    hand_send.at[2, turn], start_recv.at[1], (target, up),
+
+            @pl.when(jnp.logical_not(upper_core))
+            def _():
+                act(
+                    remote(
+                        third.at[:, :, own_last, :], third.at[:, :, upper, :],
+                        hand_send.at[1, turn], start_recv.at[0], (target, down),
+                    )
                 )
-            )
+
             return carry
 
         lax.fori_loop(0, handed, one, 0)
@@ -399,7 +438,8 @@
                 part,
                 dma((2,)), dma((2,)), dma((2,)), dma((2,)), dma((2,)), dma((2,)),
                 dma((2,)), dma((2,)), dma((times,)), dma((times,)), dma((2, times)), dma((2, times)),
-                dma((2,)), dma((2,)), dma((3, 4)), dma,
+                dma((2,)), dma((2,)), dma((2, 4)), dma, dma,
+                pltpu.SemaphoreType.REGULAR((4,)),
             ],
             compiler_params=pltpu.CompilerParams(collective_id=0, has_side_effects=True),
             cost_estimate=pl.CostEstimate(flops=100_000_000, bytes_accessed=1_000_000, transcendentals=0),

time: 52.6 us -> 50.4 us (0.958)
  Pallas kernels: 50.5 us -> 48.4 us
    pallas_call x1, Pallas kernels: 50.5 us -> 48.4 us  [body(): pl.pallas_call(functools.partial(kernel, times, strips, rows), out_shape=...]
where the time goes in v4:
time: 50.4 us; the launch traced here: 50.3 us
  Pallas kernels  48.4 us (96%)
  local copies, waits for them, and re-layouts  1.27 us (3%)
  between operations  0.64 us (1%)
    pallas_call x1, Pallas kernels, body(): pl.pallas_call(functools.partial(kernel, times, strips, rows), out_shape=...  48.4 us
    unnamed x2, local copies, waits for them, and re-layouts  1.27 us

profile of v4, /device:TPU:24, one launch (start us, length us, event | category | flops | bytes accessed | tf_op | source)
XLA Modules:
  0.0 50.3 jit_solution(4299841852844059860)
XLA Ops:
  0.6 48.4 %shard_map.50 = (f32[1,3,24,256]{3,2,1,0:T(8,128)S(1)}, f32[1,3,24,256]{3,2,1,0:T(8,128)S(1)}) custom-call(f32[3,24,256]{2,1,0:T(8,128)} %init_ref.1, f32[1,3,24,256]{3,2,1,0:T(8,128)} %guess_ref.1, f32[24,256]{1,0:T(8,128)} %fric_ref.1), custom_call_target="tpu_custom_call" | custom-call | flops 100000000 | bytes 1000000 | tf_op jit(solution)/shard_map/pallas_call | solution.py:426
  49.0 0.6 %copy.7 = f32[1,3,24,256]{3,2,1,0:T(8,128)} copy(f32[1,3,24,256]{3,2,1,0:T(8,128)S(1)} %get-tuple-element.2) | data formatting | bytes 147456
  49.6 0.6 %copy.8 = f32[1,3,24,256]{3,2,1,0:T(8,128)} copy(f32[1,3,24,256]{3,2,1,0:T(8,128)S(1)} %get-tuple-element.3) | data formatting | bytes 147456

commit v5 on v4

--- a/solution.py
+++ b/solution.py
@@ -65,7 +65,7 @@
     first, second, third, fourth, mid, drag_raw, drags, gained, defects, own_defect,
     halo_send, halo_recv, fric_send, fric_recv, init_send, start_recv,
     second_send, second_recv, defect_send, defect_recv, edge_send, edge_recv,
-    fourth_send, fourth_recv, hand_send, hand_recv, share_send, met,
+    fourth_send, fourth_recv, hand_send, hand_recv, share_send, met, load_sem,
 ):
     half = times // 2
     span = math.isqrt(times)
@@ -76,10 +76,9 @@
     place = lax.rem(t, half)
     slot = lax.rem(t + 2, times)
     slot_place = lax.rem(slot, half)
-    hands = (t >= half - span) & (t < half)
+    hands = t < span
     last = jnp.where(hands, half - 1, place)
     slot_end = slot // half * half + half
-    slot_low = jnp.where(slot < half, jnp.minimum(slot, half - span), slot)
     handed = half // span
 
     own = pl.ds(BASE + HALO, rows)
@@ -114,19 +113,46 @@
         greet(partner, z)
 
     is_last = t == times - 1
-    for field in range(3):
+    is_first = t == times - 2
+
+    def loads(block, ref, turn):
+        return [
+            pltpu.make_async_copy(
+                block.at[..., pl.ds(side * LANES, LANES)], ref.at[:, side, own, :], load_sem.at[turn, side]
+            )
+            for side in (0, 1)
+        ]
+
+    def each_load(act):
+        @pl.when(is_last)
+        def _():
+            for copy in loads(init_ref, first, 0):
+                act(copy)
+
+        @pl.when(jnp.logical_not(is_last))
+        def _():
+            for copy in loads(guess_ref.at[0], first, 0):
+                act(copy)
+
         for side in (0, 1):
-            cols = slice(side * LANES, (side + 1) * LANES)
-            first[field, side, own, :] = jnp.where(is_last, init_ref[field, :, cols], guess_ref[0, field, :, cols])
-    for side in (0, 1):
-        drag_raw[0, side, own, :] = fric_ref[:, side * LANES : (side + 1) * LANES]
-
-    @pl.when(t < half)
-    def _():
-        for field in range(3):
-            for part in (0, 1):
-                third[field, part, own, :] = init_ref[field, :, part * LANES : (part + 1) * LANES]
-
+            act(
+                pltpu.make_async_copy(
+                    fric_ref.at[:, pl.ds(side * LANES, LANES)], drag_raw.at[0, side, own, :], load_sem.at[1, side]
+                )
+            )
+
+        @pl.when(t < half)
+        def _():
+            for copy in loads(init_ref, third, 2):
+                act(copy)
+
+        @pl.when(is_first)
+        def _():
+            for copy in loads(init_ref, second, 2):
+                act(copy)
+
+    each_load(lambda copy: copy.start())
+    each_load(lambda copy: copy.wait())
     pl.semaphore_wait(barrier, 2 + len(partners))
 
     def tell(turn):
@@ -198,12 +224,10 @@
     fine_steps(first, STEPS - 4, full)
     fine_steps(first, 4, inner)
 
-    is_first = t == times - 2
-    for field in range(3):
-        for side in (0, 1):
-            second[field, side, own, :] = jnp.where(
-                is_first, init_ref[field, :, side * LANES : (side + 1) * LANES], first[field, side, own, :]
-            )
+    @pl.when(jnp.logical_not(is_first))
+    def _():
+        second[:, :, own, :] = first[:, :, own, :]
+
     second_edges = edges_of(second, second_send, second_recv)
     for copy in second_edges:
         copy.start()
@@ -234,9 +258,12 @@
         hear(3)
     d_own = pl.ds(HALO, rows)
 
+    slot_low = jnp.maximum(slot, jnp.where(slot < half, span, 0))
+    fronts = jnp.where(slot < half, span, 0)
+
     def each_defect(act):
         def one(turn, carry):
-            target = slot_end - 1 - turn
+            target = jnp.where(turn < fronts, turn, slot_end - 1 - (turn - fronts))
 
             @pl.when(target != t)
             def _():
@@ -249,10 +276,10 @@
 
             return carry
 
-        lax.fori_loop(0, slot_end - slot_low, one, 0)
+        lax.fori_loop(0, fronts + slot_end - slot_low, one, 0)
 
     each_defect(lambda copy: copy.start())
-    keeps = (t >= slot_low) & (t < slot_end)
+    keeps = ((t >= slot_low) & (t < slot_end)) | (t < fronts)
 
     @pl.when(keeps)
     def _():
@@ -356,13 +383,15 @@
             for part in (0, 1):
                 c_ref[0, field, :, part * LANES : (part + 1) * LANES] = third[field, part, own, :]
 
-    chain(inner)(place, 0)
+    lax.fori_loop(place, jnp.minimum(place + 1, wide), chain(full), 0)
+    lax.fori_loop(jnp.maximum(place, wide), place + 1, chain(inner), 0)
     put_out()
-    lax.fori_loop(place + 1, last + 1, chain(inner), 0)
+    lax.fori_loop(place + 1, jnp.minimum(last + 1, wide), chain(full), 0)
+    lax.fori_loop(jnp.maximum(place + 1, wide), last + 1, chain(inner), 0)
 
     def each_hand(act):
         def one(turn, carry):
-            target = t + span * turn + span
+            target = t + times - span - span * turn
             act(remote(third.at[:, :, own, :], third.at[:, :, own, :], hand_send.at[0, turn], hand_recv, (target, z)))
 
             @pl.when(upper_core)
@@ -426,7 +455,7 @@
         return pl.pallas_call(
             functools.partial(kernel, times, strips, rows),
             out_shape=(shape, shape),
-            in_specs=[vmem] * 3,
+            in_specs=[pl.BlockSpec(memory_space=pl.ANY)] * 3,
             out_specs=(vmem, vmem),
             scratch_shapes=[
                 state, state,
@@ -439,7 +468,7 @@
                 dma((2,)), dma((2,)), dma((2,)), dma((2,)), dma((2,)), dma((2,)),
                 dma((2,)), dma((2,)), dma((times,)), dma((times,)), dma((2, times)), dma((2, times)),
                 dma((2,)), dma((2,)), dma((2, 4)), dma, dma,
-                pltpu.SemaphoreType.REGULAR((4,)),
+                pltpu.SemaphoreType.REGULAR((4,)), dma((3, 2)),
             ],
             compiler_params=pltpu.CompilerParams(collective_id=0, has_side_effects=True),
             cost_estimate=pl.CostEstimate(flops=100_000_000, bytes_accessed=1_000_000, transcendentals=0),

time: 50.4 us -> 48.1 us (0.954)
  Pallas kernels: 48.4 us -> 46 us
    pallas_call x1, Pallas kernels: 48.4 us -> 46 us  [body(): pl.pallas_call(functools.partial(kernel, times, strips, rows), out_shape=...]
where the time goes in v5:
time: 48.1 us; the launch traced here: 47.9 us
  Pallas kernels  46 us (96%)
  local copies, waits for them, and re-layouts  1.27 us (3%)
  between operations  0.64 us (1%)
    pallas_call x1, Pallas kernels, body(): pl.pallas_call(functools.partial(kernel, times, strips, rows), out_shape=...  46 us
    unnamed x2, local copies, waits for them, and re-layouts  1.27 us

profile of v5, /device:TPU:24, one launch (start us, length us, event | category | flops | bytes accessed | tf_op | source)
XLA Modules:
  0.0 47.9 jit_solution(17392352984088075848)
XLA Ops:
  0.6 46.0 %shard_map.50 = (f32[1,3,24,256]{3,2,1,0:T(8,128)S(1)}, f32[1,3,24,256]{3,2,1,0:T(8,128)S(1)}) custom-call(f32[3,24,256]{2,1,0:T(8,128)} %init_ref.1, f32[1,3,24,256]{3,2,1,0:T(8,128)} %guess_ref.1, f32[24,256]{1,0:T(8,128)} %fric_ref.1), custom_call_target="tpu_custom_call" | custom-call | flops 100000000 | bytes 1000000 | tf_op jit(solution)/shard_map/pallas_call | solution.py:455
  46.6 0.6 %copy.7 = f32[1,3,24,256]{3,2,1,0:T(8,128)} copy(f32[1,3,24,256]{3,2,1,0:T(8,128)S(1)} %get-tuple-element.2) | data formatting | bytes 147456
  47.2 0.6 %copy.8 = f32[1,3,24,256]{3,2,1,0:T(8,128)} copy(f32[1,3,24,256]{3,2,1,0:T(8,128)S(1)} %get-tuple-element.3) | data formatting | bytes 147456

commit v6 on v5

--- a/solution.py
+++ b/solution.py
@@ -278,7 +278,12 @@
 
         lax.fori_loop(0, fronts + slot_end - slot_low, one, 0)
 
-    each_defect(lambda copy: copy.start())
+    late = slot >= times - 2
+
+    @pl.when(jnp.logical_not(late))
+    def _():
+        each_defect(lambda copy: copy.start())
+
     keeps = ((t >= slot_low) & (t < slot_end)) | (t < fronts)
 
     @pl.when(keeps)
@@ -324,6 +329,10 @@
 
     lax.fori_loop(0, last + 1, pass_edges, 0)
 
+    @pl.when(late)
+    def _():
+        each_defect(lambda copy: copy.start())
+
     upper_core = lax.rem(z, 2) == 0
     share_down = remote(third.at[:, :, own_last, :], third.at[:, :, upper, :], share_send, start_recv.at[0], (t, down))
     share_up = remote(third.at[:, :, own_first, :], third.at[:, :, lower, :], share_send, start_recv.at[1], (t, up))
@@ -441,6 +450,14 @@
         each_hand(lambda copy: copy.wait_send())
 
 
+def leave(c_ref, f_ref, c_out, f_out, sem):
+    copies = [pltpu.make_async_copy(c_ref, c_out, sem.at[0]), pltpu.make_async_copy(f_ref, f_out, sem.at[1])]
+    for copy in copies:
+        copy.start()
+    for copy in copies:
+        copy.wait()
+
+
 def solution(mesh):
     times, strips = mesh.shape["tm"], mesh.shape["space"]
 
@@ -452,7 +469,7 @@
         dma = pltpu.SemaphoreType.DMA
         vmem = pl.BlockSpec(memory_space=pltpu.VMEM)
         shape = pltpu.VMEM(c_guess.shape, jnp.float32)
-        return pl.pallas_call(
+        results = pl.pallas_call(
             functools.partial(kernel, times, strips, rows),
             out_shape=(shape, shape),
             in_specs=[pl.BlockSpec(memory_space=pl.ANY)] * 3,
@@ -473,6 +490,11 @@
             compiler_params=pltpu.CompilerParams(collective_id=0, has_side_effects=True),
             cost_estimate=pl.CostEstimate(flops=100_000_000, bytes_accessed=1_000_000, transcendentals=0),
         )(initial_state, c_guess, friction)
+        whole = jax.ShapeDtypeStruct(c_guess.shape, jnp.float32)
+        hbm = pl.BlockSpec(memory_space=pl.ANY)
+        return pl.pallas_call(
+            leave, out_shape=(whole, whole), in_specs=[vmem] * 2, out_specs=(hbm, hbm), scratch_shapes=[dma((2,))]
+        )(*[pltpu.with_memory_space_constraint(result, pltpu.VMEM) for result in results])
 
     return jax.shard_map(
         body,

time: 48.1 us -> 47.5 us (0.988)
  local copies, waits for them, and re-layouts: 1.27 us -> 0 us
  Pallas kernels: 46 us -> 46.6 us
    unnamed x2 -> x0, local copies, waits for them, and re-layouts: 1.27 us -> none
    pallas_call x0 -> x1, Pallas kernels: none -> 0.68 us  [body(): pl.pallas_call(leave, out_shape=(whole, whole), in_specs=[vmem] * 2, out_...]
where the time goes in v6:
time: 47.5 us; the launch traced here: 47.3 us
  Pallas kernels  46.6 us (98%)
  between operations  0.64 us (1%)
    pallas_call x1, Pallas kernels, body(): pl.pallas_call(functools.partial(kernel, times, strips, rows), out_shape=...  46 us

profile of v6, /device:TPU:24, one launch (start us, length us, event | category | flops | bytes accessed | tf_op | source)
XLA Modules:
  0.0 47.3 jit_solution(4015189545520253954)
XLA Ops:
  0.6 46.0 %shard_map.50 = (f32[1,3,24,256]{3,2,1,0:T(8,128)S(1)}, f32[1,3,24,256]{3,2,1,0:T(8,128)S(1)}) custom-call(f32[3,24,256]{2,1,0:T(8,128)} %init_ref.1, f32[1,3,24,256]{3,2,1,0:T(8,128)} %guess_ref.1, f32[24,256]{1,0:T(8,128)} %fric_ref.1), custom_call_target="tpu_custom_call" | custom-call | flops 100000000 | bytes 1000000 | tf_op jit(solution)/shard_map/pallas_call | solution.py:472
  46.6 0.7 %shard_map.51 = (f32[1,3,24,256]{3,2,1,0:T(8,128)}, f32[1,3,24,256]{3,2,1,0:T(8,128)}) custom-call(f32[1,3,24,256]{3,2,1,0:T(8,128)S(1)} %get-tuple-element.4.c_ref, f32[1,3,24,256]{3,2,1,0:T(8,128)S(1)} %get-tuple-element.5.f_ref), custom_call_target="tpu_custom_call" | custom-call | tf_op jit(solution)/shard_map/pallas_call | solution.py:495

commit v7 on v6

--- a/solution.py
+++ b/solution.py
@@ -141,6 +141,7 @@
                 )
             )
 
+    def each_late_load(act):
         @pl.when(t < half)
         def _():
             for copy in loads(init_ref, third, 2):
@@ -152,6 +153,7 @@
                 act(copy)
 
     each_load(lambda copy: copy.start())
+    each_late_load(lambda copy: copy.start())
     each_load(lambda copy: copy.wait())
     pl.semaphore_wait(barrier, 2 + len(partners))
 
@@ -167,6 +169,7 @@
     third_edges = edges_of(third, init_send, start_recv)
     for copy in first_edges + drag_edges:
         copy.start()
+    each_late_load(lambda copy: copy.wait())
 
     @pl.when(t < half)
     def _():
@@ -208,21 +211,33 @@
 
         lax.fori_loop(0, count, step, 0)
 
+    def last_steps(state):
+        fine_steps(state, 3, inner)
+
+        def put(field, side, row, value):
+            state[field, side, pl.ds(row, 8), :] = value
+
+        half_step(state, 0, time_step, inner)
+        end_step(state, 0, time_step, strip, put)
+
+    def set_drags(chunks):
+        for row in chunks:
+            for side in (0, 1):
+                base = 2.0 * drag_raw[0, side, pl.ds(row, 8), :] + 4.0
+                for kind, step in ((0, time_step), (2, coarse_step)):
+                    drags[kind, side, pl.ds(row, 8), :] = 1.0 - (0.5 * step) * base
+                    drags[kind + 1, side, pl.ds(row, 8), :] = 0.5 - (0.25 * step) * base
+
+    set_drags(strip)
     for copy in first_edges + drag_edges:
         copy.wait()
-    for row in full:
-        for side in (0, 1):
-            base = 2.0 * drag_raw[0, side, pl.ds(row, 8), :] + 4.0
-            for kind, step in ((0, time_step), (2, coarse_step)):
-                drags[kind, side, pl.ds(row, 8), :] = 1.0 - (0.5 * step) * base
-                drags[kind + 1, side, pl.ds(row, 8), :] = 0.5 - (0.25 * step) * base
-
+    set_drags([row for row in full if row not in strip])
     hear(0)
     if len(partners) > 1:
         tell(1)
 
     fine_steps(first, STEPS - 4, full)
-    fine_steps(first, 4, inner)
+    last_steps(first)
 
     @pl.when(jnp.logical_not(is_first))
     def _():
@@ -251,7 +266,7 @@
     for copy in second_edges:
         copy.wait_send()
     fine_steps(second, STEPS - 4, full)
-    fine_steps(second, 4, inner)
+    last_steps(second)
     own_defect[...] = second[:, :, own, :] - gained[...]
 
     if len(partners) > 3:
@@ -432,7 +447,7 @@
     for copy in fourth_edges:
         copy.wait()
     fine_steps(fourth, STEPS - 5, full)
-    fine_steps(fourth, 4, inner)
+    last_steps(fourth)
     for field in range(3):
         for side in (0, 1):
             f_ref[0, field, :, side * LANES : (side + 1) * LANES] = fourth[field, side, own, :]

time: 47.5 us -> 47.8 us (level)
  no operation moved by 1% of the time
where the time goes in v7:
time: 47.8 us; the launch traced here: 47.2 us
  Pallas kernels  46.6 us (97%)
  between operations  0.64 us (1%)
    pallas_call x1, Pallas kernels, body(): pl.pallas_call(functools.partial(kernel, times, strips, rows), out_shape=...  45.9 us

profile of v7, /device:TPU:24, one launch (start us, length us, event | category | flops | bytes accessed | tf_op | source)
XLA Modules:
  0.0 47.2 jit_solution(11528701796941634513)
XLA Ops:
  0.6 45.9 %shard_map.50 = (f32[1,3,24,256]{3,2,1,0:T(8,128)S(1)}, f32[1,3,24,256]{3,2,1,0:T(8,128)S(1)}) custom-call(f32[3,24,256]{2,1,0:T(8,128)} %init_ref.1, f32[1,3,24,256]{3,2,1,0:T(8,128)} %guess_ref.1, f32[24,256]{1,0:T(8,128)} %fric_ref.1), custom_call_target="tpu_custom_call" | custom-call | flops 100000000 | bytes 1000000 | tf_op jit(solution)/shard_map/pallas_call | solution.py:487
  46.5 0.7 %shard_map.51 = (f32[1,3,24,256]{3,2,1,0:T(8,128)}, f32[1,3,24,256]{3,2,1,0:T(8,128)}) custom-call(f32[1,3,24,256]{3,2,1,0:T(8,128)S(1)} %get-tuple-element.4.c_ref, f32[1,3,24,256]{3,2,1,0:T(8,128)S(1)} %get-tuple-element.5.f_ref), custom_call_target="tpu_custom_call" | custom-call | tf_op jit(solution)/shard_map/pallas_call | solution.py:510
